TPU v7x, 16 devices: a whole 2x2x2 slice. The times are simulated.
16 devices in a mesh: row: 2 (over z), col: 8 (over y, x, core).
Axes of the slice: x: 2, y: 2, z: 2, core: 2. Of those that a mesh axis runs over, the one named last changes fastest.
Arguments:
- w_one: float32 [2, 8, 4, 512, 2048], P('row', 'col')
- w_two: float32 [2, 8, 4, 2048, 512], P('row', 'col')
- inputs: bfloat16 [2, 8, 3, 1024, 512], P('row', 'col')
- targets: bfloat16 [2, 8, 3, 1024, 512], P('row', 'col')
Outputs:
- output 1: float32 [2, 8, 4, 512, 2048], P('row', 'col')
- output 2: float32 [2, 8, 4, 2048, 512], P('row', 'col')
All inputs are finite; a program needn't handle non-finite values.
Results may differ from a plain program's by a relative error of at most 0.00197.
Values are sent between devices in bfloat16 or wider.
A program may use at most 1 GiB of HBM per device.

v0:
```python
import functools

import jax
import jax.numpy as jnp
from jax import lax
from jax.experimental import pallas as pl
from jax.experimental.pallas import tpu as pltpu
from jax.sharding import PartitionSpec as P


LEARN_RATE = 1.5
NORM_EPS = 1e-6
GELU_C = 0.7978845608028654
GELU_K = 0.044715
TILE = 512
ROWS = 1024
F32 = jnp.float32
BF16 = jnp.bfloat16


def gelu_value(z):
    tanh_inner = jnp.tanh(z * (GELU_C + (GELU_C * GELU_K) * (z * z)))
    half = 0.5 * z
    return half + half * tanh_inner


def gelu_both(z):
    sq = z * z
    tanh_inner = jnp.tanh(z * (GELU_C + (GELU_C * GELU_K) * sq))
    half = 0.5 * z
    value = half + half * tanh_inner
    slope = (0.5 + 0.5 * tanh_inner) + (half * (1.0 - tanh_inner * tanh_inner)) * (GELU_C + (3.0 * GELU_C * GELU_K) * sq)
    return value, slope


def mm(a, b, dims=((1,), (0,))):
    return lax.dot_general(a, b, (dims, ((), ())), preferred_element_type=F32)


NT = ((1,), (1,))
TN = ((0,), (0,))


def inv_rms_of(x):
    return lax.rsqrt(jnp.mean(x * x, axis=-1, keepdims=True) + NORM_EPS)


def norm_back(x, m):
    inv = inv_rms_of(x)
    n = x * inv
    return inv * (m - n * jnp.mean(m * n, axis=-1, keepdims=True))


def row_blocks(n):
    return [slice(k, k + ROWS) for k in range(0, n, ROWS)]


def params(mib=48):
    return pltpu.CompilerParams(dimension_semantics=('arbitrary',), vmem_limit_bytes=mib << 20)


def cost(flops, nbytes, trans=0):
    return pl.CostEstimate(flops=flops, bytes_accessed=nbytes, transcendentals=trans)


def fwd_body(h_ref, w1_ref, w2_ref, hn_ref, n_scr, acc_scr):
    j = pl.program_id(0)
    blocks = row_blocks(h_ref.shape[0])

    @pl.when(j == 0)
    def _():
        for r in blocks:
            x = h_ref[r, :].astype(F32)
            n_scr[r, :] = (x * inv_rms_of(x)).astype(BF16)
            acc_scr[r, :] = jnp.zeros((ROWS, acc_scr.shape[1]), F32)

    w1 = w1_ref[...].astype(BF16)
    w2 = w2_ref[...].astype(BF16)
    for r in blocks:
        a = gelu_value(mm(n_scr[r, :], w1)).astype(BF16)
        acc_scr[r, :] += mm(a, w2)

    @pl.when(j == pl.num_programs(0) - 1)
    def _():
        for r in blocks:
            hn_ref[r, :] = (h_ref[r, :].astype(F32) + acc_scr[r, :]).astype(BF16)


def fwd_layer(h, hk, w1, k1, w2, k2):
    b, d = h.shape[1:]
    f = w1.shape[2]
    return pl.pallas_call(
        fwd_body, grid=(f // TILE,), name='fwd',
        in_specs=[pl.BlockSpec((None, b, d), lambda j: (hk, 0, 0)), pl.BlockSpec((None, d, TILE), lambda j: (k1, 0, j)),
                  pl.BlockSpec((None, TILE, d), lambda j: (k2, j, 0))],
        out_specs=pl.BlockSpec((b, d), lambda j: (0, 0)), out_shape=jax.ShapeDtypeStruct((b, d), BF16),
        scratch_shapes=[pltpu.VMEM((b, d), BF16), pltpu.VMEM((b, d), F32)], compiler_params=params(),
        cost_estimate=cost(4 * b * d * f, 8 * d * f + 4 * b * d, b * f))(h, w1, w2)


def chain_body(n_fwd, nt, mixing, loss_scale, *refs):
    refs = list(refs)
    h_ref, hist_ref = refs.pop(0), None
    w1f_ref = refs.pop(0)
    w2f_refs = [refs.pop(0) for _ in range(4 if mixing else 1)]
    t_ref, w1h_ref, w2h_ref = [refs.pop(0) for _ in range(3)]
    hist_ref, a_ref, e_ref, q_ref, wire_ref = [refs.pop(0) for _ in range(5)]
    if mixing:
        p_ref = refs.pop(0)
    h_scr, n_scr, acc_scr, a_scr, w_scr, elo_scr = refs
    i = pl.program_id(0)
    j = lax.rem(i, nt)
    in_fwd = i < n_fwd * nt
    in_head = (i >= n_fwd * nt) & (i < (n_fwd + 1) * nt)
    b = h_ref.shape[0]
    half = e_ref.shape[1]
    blocks = row_blocks(b)

    @pl.when(i == 0)
    def _():
        h_scr[...] = h_ref[...]

    @pl.when((j == 0) & (i <= n_fwd * nt))
    def _():
        for r in blocks:
            x = h_scr[r, :].astype(F32)
            n_scr[r, :] = (x * inv_rms_of(x)).astype(BF16)
        acc_scr[...] = jnp.zeros_like(acc_scr)

    @pl.when(in_fwd)
    def _():
        w1 = w1f_ref[...].astype(BF16)
        if mixing:
            w2 = mix_vals(*[w[...] for w in w2f_refs])
            p_ref[...] = w2
        else:
            w2 = w2f_refs[0][...]
        w2 = w2.astype(BF16)
        for r in blocks:
            a = gelu_value(mm(n_scr[r, :], w1)).astype(BF16)
            acc_scr[r, :] += mm(a, w2)

    @pl.when(in_fwd & (j == nt - 1))
    def _():
        for r in blocks:
            out = (h_scr[r, :].astype(F32) + acc_scr[r, :]).astype(BF16)
            h_scr[r, :] = out
            hist_ref[r, :] = out

    @pl.when(in_head)
    def _():
        w1 = w1h_ref[...].astype(BF16)
        w2 = w2h_ref[...]
        w_scr[j] = w2
        w2 = w2.astype(BF16)
        for r in blocks:
            a = gelu_value(mm(n_scr[r, :], w1)).astype(BF16)
            a_scr[j, r, :] = a
            a_ref[r, :] = a
            acc_scr[r, :half] += mm(a, w2)

    @pl.when(in_head & (j == nt - 1))
    def _():
        for r in blocks:
            out = (h_scr[r, :half].astype(F32) + acc_scr[r, :half]).astype(BF16)
            e = loss_scale * (out.astype(F32) - t_ref[r, :].astype(F32))
            e_ref[r, :] = e
            elo_scr[r, :] = e.astype(BF16)

    @pl.when(i >= (n_fwd + 1) * nt)
    def _():
        q = w_scr[j] - LEARN_RATE * mm(a_scr[j], elo_scr[...], TN)
        q_ref[...] = q
        wire_ref[...] = q.astype(BF16)


def chain(n_fwd, h, hk, target, tk, w1f, k1f, w2f, k2f, w1h, k1h, w2h, k2h, half, loss_scale):
    b, d = h.shape[1:]
    f = w1f.shape[2]
    nt = f // TILE
    mixing = isinstance(w2f, tuple)
    n_steps = n_fwd * nt

    def f_layer(i):
        return jnp.minimum(i, n_steps - 1) // nt

    def f_tile(i):
        return jnp.minimum(i, n_steps - 1) % nt

    def h_tile(i):
        return jnp.clip(i - n_steps, 0, nt - 1)

    def g_tile(i):
        return jnp.maximum(i - n_steps - nt, 0)

    in_specs = [pl.BlockSpec((None, b, d), lambda i: (hk, 0, 0)),
                pl.BlockSpec((None, d, TILE), lambda i: (k1f + f_layer(i), 0, f_tile(i)))]
    if mixing:
        in_specs += [pl.BlockSpec((TILE, d), lambda i: (f_tile(i), 0))] * 4
    else:
        in_specs.append(pl.BlockSpec((None, TILE, d), lambda i: (k2f + f_layer(i), f_tile(i), 0)))
    in_specs += [pl.BlockSpec((None, b, half), lambda i: (tk, 0, 0)), pl.BlockSpec((None, d, TILE), lambda i: (k1h, 0, h_tile(i))),
                 pl.BlockSpec((None, TILE, half), lambda i: (k2h, h_tile(i), 0))]
    out_specs = [pl.BlockSpec((None, b, d), lambda i: (f_layer(i), 0, 0)), pl.BlockSpec((b, TILE), lambda i: (0, h_tile(i))),
                 pl.BlockSpec((b, half), lambda i: (0, 0))] + [pl.BlockSpec((TILE, half), lambda i: (g_tile(i), 0))] * 2
    out_shape = [jax.ShapeDtypeStruct((n_fwd, b, d), BF16), jax.ShapeDtypeStruct((b, f), BF16), jax.ShapeDtypeStruct((b, half), F32),
                 jax.ShapeDtypeStruct((f, half), F32), jax.ShapeDtypeStruct((f, half), BF16)]
    if mixing:
        out_specs.append(pl.BlockSpec((TILE, d), lambda i: (f_tile(i), 0)))
        out_shape.append(jax.ShapeDtypeStruct((f, d), F32))
    return pl.pallas_call(
        functools.partial(chain_body, n_fwd, nt, mixing, loss_scale), grid=((n_fwd + 2) * nt,), name='chain',
        in_specs=in_specs, out_specs=out_specs, out_shape=out_shape,
        scratch_shapes=[pltpu.VMEM((b, d), BF16), pltpu.VMEM((b, d), BF16), pltpu.VMEM((b, d), F32), pltpu.VMEM((nt, b, TILE), BF16),
                        pltpu.VMEM((nt, TILE, half), F32), pltpu.VMEM((b, half), BF16)],
        compiler_params=params(),
        cost_estimate=cost(2 * b * f * (2 * n_fwd * d + d + 2 * half), 8 * n_fwd * d * f + 4 * d * f + 2 * b * f + 10 * f * half, (n_fwd + 1) * b * f))(
            h, w1f, *(w2f if mixing else (w2f,)), target, w1h, w2h)


def tail_body(nt, mixing, loss_scale, *refs):
    refs = list(refs)
    a_ref, h_ref, hc_ref, t_ref, e0_ref, w1_ref, w20_ref = [refs.pop(0) for _ in range(7)]
    w21_refs = [refs.pop(0) for _ in range(4 if mixing else 1)]
    e1_ref, dz_ref, q_ref, wire_ref = [refs.pop(0) for _ in range(4)]
    if mixing:
        p_ref = refs.pop(0)
    n_scr, acc_scr, w2_scr, elo_scr = refs
    i = pl.program_id(0)
    j = lax.rem(i, nt)
    blocks = row_blocks(h_ref.shape[0])
    half = e0_ref.shape[1]

    @pl.when(i == 0)
    def _():
        acc_scr[...] = jnp.zeros_like(acc_scr)
        for r in blocks:
            x = h_ref[r, :].astype(F32)
            n_scr[r, :] = (x * inv_rms_of(x)).astype(BF16)

    @pl.when(i < nt)
    def _():
        if mixing:
            w2 = mix_vals(*[w[...] for w in w21_refs])
            p_ref[...] = w2
        else:
            w2 = w21_refs[0][...]
        w2 = w2.astype(BF16)
        w2_scr[j, :, :half] = w20_ref[...].astype(BF16)
        w2_scr[j, :, half:] = w2
        acc_scr[...] += mm(a_ref[...], w2)

    @pl.when(i == nt - 1)
    def _():
        for r in blocks:
            out = (hc_ref[r, :].astype(F32) + acc_scr[r, :]).astype(BF16)
            e = loss_scale * (out.astype(F32) - t_ref[r, :].astype(F32))
            e1_ref[r, :] = e
            elo_scr[r, :half] = e0_ref[r, :].astype(BF16)
            elo_scr[r, half:] = e.astype(BF16)

    @pl.when(i >= nt)
    def _():
        w1 = w1_ref[...]
        w1_lo = w1.astype(BF16)
        for r in blocks:
            _, slope = gelu_both(mm(n_scr[r, :], w1_lo))
            dz_ref[r, :] = (mm(elo_scr[r, :], w2_scr[j], NT) * slope).astype(BF16)
        q = w1 - LEARN_RATE * mm(n_scr[...], dz_ref[...], TN)
        q_ref[...] = q
        wire_ref[...] = q.astype(BF16)


def tail(act, h, hk, target, tk, e0, w1, k1, w20, k20, w21, k21, c21, half, loss_scale):
    b, d = h.shape[1:]
    f = w1.shape[2]
    nt = f // TILE
    mixing = isinstance(w21, tuple)

    def p_tile(i):
        return jnp.minimum(i, nt - 1)

    def g_tile(i):
        return jnp.maximum(i - nt, 0)

    in_specs = [pl.BlockSpec((b, TILE), lambda i: (0, p_tile(i))), pl.BlockSpec((None, b, d), lambda i: (hk, 0, 0)),
                pl.BlockSpec((None, b, half), lambda i: (hk, 0, 1)), pl.BlockSpec((None, b, half), lambda i: (tk, 0, 1)),
                pl.BlockSpec((b, half), lambda i: (0, 0)), pl.BlockSpec((None, d, TILE), lambda i: (k1, 0, g_tile(i))),
                pl.BlockSpec((None, TILE, half), lambda i: (k20, p_tile(i), 0))]
    if mixing:
        in_specs += [pl.BlockSpec((TILE, half), lambda i: (p_tile(i), 0))] * 4
    else:
        in_specs.append(pl.BlockSpec((None, TILE, half), lambda i: (k21, p_tile(i), c21)))
    out_specs = [pl.BlockSpec((b, half), lambda i: (0, 0)), pl.BlockSpec((b, TILE), lambda i: (0, g_tile(i)))]
    out_specs += [pl.BlockSpec((d, TILE), lambda i: (0, g_tile(i)))] * 2
    out_shape = [jax.ShapeDtypeStruct((b, half), F32), jax.ShapeDtypeStruct((b, f), BF16), jax.ShapeDtypeStruct((d, f), F32),
                 jax.ShapeDtypeStruct((d, f), BF16)]
    if mixing:
        out_specs.append(pl.BlockSpec((TILE, half), lambda i: (p_tile(i), 0)))
        out_shape.append(jax.ShapeDtypeStruct((f, half), F32))
    return pl.pallas_call(
        functools.partial(tail_body, nt, mixing, loss_scale), grid=(2 * nt,), name='tail', in_specs=in_specs, out_specs=out_specs,
        out_shape=out_shape,
        scratch_shapes=[pltpu.VMEM((b, d), BF16), pltpu.VMEM((b, half), F32), pltpu.VMEM((nt, TILE, d), BF16), pltpu.VMEM((b, d), BF16)],
        compiler_params=params(),
        cost_estimate=cost(2 * b * f * (3 * d + half), 10 * d * f + 8 * f * half + 4 * b * f, b * f))(
            act, h, h, target, e0, w1, w20, *(w21 if mixing else (w21,)))


def last_body(a_ref, dz_ref, h_ref, e0_ref, e1_ref, w1_ref, w2_ref, q_ref, wire_ref, en_ref, m_scr, elo_scr):
    j = pl.program_id(0)
    blocks = row_blocks(h_ref.shape[0])
    half = e0_ref.shape[1]

    @pl.when(j == 0)
    def _():
        m_scr[...] = jnp.zeros_like(m_scr)
        elo_scr[...] = e1_ref[...].astype(BF16)

    m_scr[...] += mm(dz_ref[...], w1_ref[...].astype(BF16), NT)
    q = w2_ref[...] - LEARN_RATE * mm(a_ref[...], elo_scr[...], TN)
    q_ref[...] = q
    wire_ref[...] = q.astype(BF16)

    @pl.when(j == pl.num_programs(0) - 1)
    def _():
        for r in blocks:
            step = norm_back(h_ref[r, :].astype(F32), m_scr[r, :])
            en_ref[r, :half] = e0_ref[r, :] + step[:, :half]
            en_ref[r, half:] = e1_ref[r, :] + step[:, half:]


def bwd_last(act, dz, h, hk, e0, e1, w1, k1, w2, k2, c2, half):
    b, d = h.shape[1:]
    f = w1.shape[2]
    return pl.pallas_call(
        last_body, grid=(f // TILE,), name='bwd_last',
        in_specs=[pl.BlockSpec((b, TILE), lambda j: (0, j))] * 2 + [pl.BlockSpec((None, b, d), lambda j: (hk, 0, 0))]
        + [pl.BlockSpec((b, half), lambda j: (0, 0))] * 2
        + [pl.BlockSpec((None, d, TILE), lambda j: (k1, 0, j)), pl.BlockSpec((None, TILE, half), lambda j: (k2, j, c2))],
        out_specs=[pl.BlockSpec((TILE, half), lambda j: (j, 0))] * 2 + [pl.BlockSpec((b, d), lambda j: (0, 0))],
        out_shape=[jax.ShapeDtypeStruct((f, half), F32), jax.ShapeDtypeStruct((f, half), BF16), jax.ShapeDtypeStruct((b, d), F32)],
        scratch_shapes=[pltpu.VMEM((b, d), F32), pltpu.VMEM((b, half), BF16)], compiler_params=params(),
        cost_estimate=cost(2 * b * f * (d + half), 4 * d * f + 10 * f * half + 4 * b * f))(act, dz, h, e0, e1, w1, w2)


def bwd_body(with_next, e_ref, h_ref, w1_ref, w2_ref, q1_ref, wire1_ref, q2_ref, wire2_ref, *rest):
    if with_next:
        en_ref, elo_scr, n_scr, a_scr, dz_scr, m_scr = rest
    else:
        elo_scr, n_scr, a_scr, dz_scr = rest
    j = pl.program_id(0)
    blocks = row_blocks(h_ref.shape[0])

    @pl.when(j == 0)
    def _():
        for r in blocks:
            elo_scr[r, :] = e_ref[r, :].astype(BF16)
            x = h_ref[r, :].astype(F32)
            n_scr[r, :] = (x * inv_rms_of(x)).astype(BF16)
        if with_next:
            m_scr[...] = jnp.zeros_like(m_scr)

    w1 = w1_ref[...].astype(BF16)
    w2 = w2_ref[...].astype(BF16)
    for r in blocks:
        value, slope = gelu_both(mm(n_scr[r, :], w1))
        a_scr[r, :] = value.astype(BF16)
        dz = (mm(elo_scr[r, :], w2, NT) * slope).astype(BF16)
        dz_scr[r, :] = dz
        if with_next:
            m_scr[r, :] += mm(dz, w1, NT)
    q1 = w1_ref[...] - LEARN_RATE * mm(n_scr[...], dz_scr[...], TN)
    q1_ref[...] = q1
    wire1_ref[...] = q1.astype(BF16)
    q2 = w2_ref[...] - LEARN_RATE * mm(a_scr[...], elo_scr[...], TN)
    q2_ref[...] = q2
    wire2_ref[...] = q2.astype(BF16)

    if with_next:
        @pl.when(j == pl.num_programs(0) - 1)
        def _():
            for r in blocks:
                en_ref[r, :] = e_ref[r, :] + norm_back(h_ref[r, :].astype(F32), m_scr[r, :])


def bwd_layer(e, h, hk, w1, k1, w2, k2, with_next):
    b, d = h.shape[1:]
    f = w1.shape[2]
    out_specs = [pl.BlockSpec((d, TILE), lambda j: (0, j))] * 2 + [pl.BlockSpec((TILE, d), lambda j: (j, 0))] * 2
    out_shape = [jax.ShapeDtypeStruct((d, f), F32), jax.ShapeDtypeStruct((d, f), BF16),
                 jax.ShapeDtypeStruct((f, d), F32), jax.ShapeDtypeStruct((f, d), BF16)]
    scratch = [pltpu.VMEM((b, d), BF16), pltpu.VMEM((b, d), BF16), pltpu.VMEM((b, TILE), BF16), pltpu.VMEM((b, TILE), BF16)]
    if with_next:
        out_specs.append(pl.BlockSpec((b, d), lambda j: (0, 0)))
        out_shape.append(jax.ShapeDtypeStruct((b, d), F32))
        scratch.append(pltpu.VMEM((b, d), F32))
    n_mm = 5 if with_next else 4
    return pl.pallas_call(
        functools.partial(bwd_body, with_next), grid=(f // TILE,), name='bwd_mid' if with_next else 'bwd_first',
        in_specs=[pl.BlockSpec((b, d), lambda j: (0, 0)), pl.BlockSpec((None, b, d), lambda j: (hk, 0, 0)),
                  pl.BlockSpec((None, d, TILE), lambda j: (k1, 0, j)), pl.BlockSpec((None, TILE, d), lambda j: (k2, j, 0))],
        out_specs=out_specs, out_shape=out_shape, scratch_shapes=scratch, compiler_params=params(),
        cost_estimate=cost(2 * n_mm * b * d * f, 20 * d * f, b * f))(e, h, w1, w2)


def mix_vals(own, prev, nxt, row):
    row = row.astype(F32)
    return (own + prev.astype(F32) + nxt.astype(F32) + row + row) / 5.0


def place_body(n_alias, own_ref, prev_ref, nxt_ref, row_ref, *rest):
    out_ref = rest[n_alias]
    out_ref[...] = mix_vals(own_ref[...], prev_ref[...], nxt_ref[...], row_ref[...])


def place(stack, shape, layer, col, own, recv):
    r, c = own.shape
    tr = r // 4
    spec = pl.BlockSpec((tr, c), lambda i: (i, 0))
    args = [own, *recv]
    in_specs = [spec] * 4
    aliases = {}
    if stack is not None:
        args.append(stack)
        in_specs.append(pl.BlockSpec(memory_space=pl.ANY))
        aliases = {4: 0}
    return pl.pallas_call(
        functools.partial(place_body, len(aliases)), grid=(4,), in_specs=in_specs,
        out_specs=pl.BlockSpec((None, tr, c), lambda i: (layer, i, col)), out_shape=jax.ShapeDtypeStruct(shape, F32),
        input_output_aliases=aliases, compiler_params=params(), name='place',
        cost_estimate=cost(5 * r * c, 14 * r * c))(*args)


def solution(mesh):
    n_rows = mesh.shape['row']
    n_cols = mesh.shape['col']
    from_col_prev = [(i, (i + 1) % n_cols) for i in range(n_cols)]
    from_col_next = [(i, (i - 1) % n_cols) for i in range(n_cols)]
    from_row = [(i, (i + 1) % n_rows) for i in range(n_rows)]

    def after(value, *others):
        return lax.optimization_barrier((value,) + others)[0]

    def send(wire):
        row = lax.ppermute(wire, 'row', from_row)
        prev = lax.ppermute(wire, 'col', from_col_prev)
        nxt = lax.ppermute(wire, 'col', from_col_next)
        return prev, nxt, row

    def device_fn(w_one, w_two, inputs, targets):
        n_layers, d, _ = w_one.shape[2:]
        last = n_layers - 1
        half = d // 2
        n_steps, b = inputs.shape[2:4]
        loss_scale = 2.0 / (b * d)
        stack_one, stack_two = w_one[0, 0], w_two[0, 0]
        x_all, t_all = inputs[0, 0], targets[0, 0]
        one = [(stack_one, k) for k in range(n_layers)]
        two = [(stack_two, k) for k in range(last)]
        halves = [(stack_two, last), (stack_two, last, 1)]
        for step in range(n_steps):
            recvs, names, own, outs = [], [], {}, {}
            final = step == n_steps - 1

            def settle(k):
                name = names[k]
                if name[0] == 'one':
                    outs['one'] = place(outs.get('one'), stack_one.shape, name[1], 0, own[name], recvs[k])
                else:
                    layer, col = (last, int(name[1])) if name[0] == 'h' else (name[1], 0)
                    outs['two'] = place(outs.get('two'), stack_two.shape, layer, col, own[name], recvs[k])

            def push(name, q, wire, gate=None):
                if gate is not None and final:
                    settle(gate)
                    kinds = sorted(outs)
                    wire, *vals = lax.optimization_barrier((wire, *recvs[gate], *[outs[k] for k in kinds]))
                    outs.update(zip(kinds, vals[3:]))
                elif gate is not None:
                    wire = after(wire, *recvs[gate])
                recvs.append(send(wire))
                names.append(name)
                own[name] = q

            hidden = [(x_all, step)]
            if step == 0:
                hist, act, e0, q, wire = chain(last, *hidden[0], t_all, step, stack_one, 0, stack_two, 0, stack_one, last, stack_two, last, half, loss_scale)
                hidden += [(hist, l) for l in range(last)]
            else:
                for l in range(last - 1):
                    hidden.append((fwd_layer(*hidden[l], *one[l], *two[l])[None], 0))
                hist, act, e0, q, wire, mixed_two = chain(1, *hidden[last - 1], t_all, step, *one[last - 1], two[last - 1], 0, *one[last], *halves[0], half, loss_scale)
                two[last - 1] = (mixed_two[None], 0)
                hidden.append((hist, 0))
            push('h0', q, wire)
            res = tail(act, *hidden[last], t_all, step, e0, *one[last], *halves[0], *halves[1], half, loss_scale)
            e1, dz = res[:2]
            push(('one', last), *res[2:4])
            if step > 0:
                halves[1] = (res[4][None], 0, 0)
            ready = {}
            q, wire, err = bwd_last(act, dz, *hidden[last], e0, e1, *one[last], *halves[1], half)
            ready['h1'] = (q, wire)
            for l in reversed(range(last)):
                res = bwd_layer(err, *hidden[l], *one[l], *two[l], l > 0)
                ready['one', l], ready['two', l] = res[0:2], res[2:4]
                if l > 0:
                    err = res[4]
            early = ('one', last - 1)
            order = [early] + [(kind, l) for l in range(last) for kind in ('one', 'two') if (kind, l) != early] + ['h1']
            for name in order:
                push(name, *ready[name], gate=len(recvs) - 2)
            if not final:
                parts = {name: (own[name], *recv) for name, recv in zip(names, recvs)}
                deferred = ('h1', ('two', last - 1))
                mixed = {name: mix_vals(*vals)[None] for name, vals in parts.items() if name not in deferred}
                one = [(mixed['one', l], 0) for l in range(n_layers)]
                two = [(mixed['two', l], 0) for l in range(last - 1)] + [parts['two', last - 1]]
                halves = [(mixed['h0'], 0), (parts['h1'], 0, 0)]
        for k in range(len(names) - 2, len(names)):
            settle(k)
        return outs['one'][None, None], outs['two'][None, None]

    grid_spec = P('row', 'col')
    return jax.shard_map(device_fn, mesh=mesh, in_specs=(grid_spec, grid_spec, grid_spec, grid_spec), out_specs=(grid_spec, grid_spec), check_vma=False)
```

profile of v0, /device:TPU:0, one launch (start us, length us, event | category | flops | bytes accessed | tf_op | source)
XLA Modules:
  0.0 1320.9 jit_solution(17806119419542562962)
XLA Ops:
  0.6 34.2 %chain.3 = (bf16[3,1024,512]{2,1,0:T(8,128)(2,1)}, bf16[1024,2048]{1,0:T(8,128)(2,1)}, f32[1024,256]{1,0:T(8,128)S(1)}, f32[2048,256]{1,0:T(8,128)S(1)}, bf16[2048,256]{1,0:T(8,128)(2,1)S(1)}) custom-call(bf16[3,1024,512]{2,1,0:T(8,128)(2,1)} %bitcast.42, f32[4,512,2048]{2,1,0:T(8,128)} %bitcast.65, f32[4,2048,512]{2,1,0:T(8,128)} %bitcast.56, ...), custom_call_target="tpu_custom_call" | custom-call | flops 17179869184 | bytes 38797312 | tf_op jit(solution)/shard_map/chain/pallas_call | solution.py:211
  34.8 17.1 %tail.3 = (f32[1024,256]{1,0:T(8,128)S(1)}, bf16[1024,2048]{1,0:T(8,128)(2,1)}, f32[512,2048]{1,0:T(8,128)}, bf16[512,2048]{1,0:T(8,128)(2,1)S(1)}) custom-call(bf16[1024,2048]{1,0:T(8,128)(2,1)} %get-tuple-element.118.refs_0_.a_ref, bf16[3,1024,512]{2,1,0:T(8,128)(2,1)} %get-tuple-element.119.refs_1_.refs_2_.h_ref, ...), custom_call_target="tpu_custom_call" | custom-call | flops 7516192768 | bytes 23068672 | tf_op jit(solution)/shard_map/tail/pallas_call | solution.py:301
  69.8 51.7 %collective-permute-done.6 = bf16[2048,256]{1,0:T(8,128)(2,1)S(1)} collective-permute-done((bf16[2048,256]{1,0:T(8,128)(2,1)S(1)}, bf16[2048,256]{1,0:T(8,128)(2,1)S(1)}, u32[]{:S(2)}, u32[]{:S(2)}) %collective-permute-start.6) | collective-permute-done | bytes 1048608 | tf_op jit(solution)/shard_map/ppermute | solution.py:447
  124.6 20.8 %bwd_mid.6 = (f32[512,2048]{1,0:T(8,128)}, bf16[512,2048]{1,0:T(8,128)(2,1)}, f32[2048,512]{1,0:T(8,128)}, bf16[2048,512]{1,0:T(8,128)(2,1)S(1)}, f32[1024,512]{1,0:T(8,128)}) custom-call(f32[1024,512]{1,0:T(8,128)} %get-tuple-element.123.e_ref, bf16[3,1024,512]{2,1,0:T(8,128)(2,1)} %get-tuple-element.119.refs_1_.refs_2_.h_ref, f32[4,512,2048]{2,1,0:T(8,128)} %bitcast.69, ...), custom_call_target="tpu_custom_call" | custom-call | flops 10737418240 | bytes 20971520 | tf_op jit(solution)/shard_map/bwd_mid/pallas_call | solution.py:399
  146.9 20.1 %bwd_mid.7 = (f32[512,2048]{1,0:T(8,128)}, bf16[512,2048]{1,0:T(8,128)(2,1)S(1)}, f32[2048,512]{1,0:T(8,128)}, bf16[2048,512]{1,0:T(8,128)(2,1)S(1)}, f32[1024,512]{1,0:T(8,128)}) custom-call(f32[1024,512]{1,0:T(8,128)} %get-tuple-element.124.e_ref, bf16[3,1024,512]{2,1,0:T(8,128)(2,1)} %get-tuple-element.119.refs_1_.refs_2_.h_ref, ...), custom_call_target="tpu_custom_call" | custom-call | flops 10737418240 | bytes 20971520 | tf_op jit(solution)/shard_map/bwd_mid/pallas_call | solution.py:399
  167.0 16.6 %bwd_first.3 = (f32[512,2048]{1,0:T(8,128)}, bf16[512,2048]{1,0:T(8,128)(2,1)S(1)}, f32[2048,512]{1,0:T(8,128)}, bf16[2048,512]{1,0:T(8,128)(2,1)S(1)}) custom-call(f32[1024,512]{1,0:T(8,128)} %get-tuple-element.125.e_ref, bf16[3,1024,512]{2,1,0:T(8,128)(2,1)} %bitcast.43, f32[4,512,2048]{2,1,0:T(8,128)} %bitcast.71, f32[4,2048,512]{2,1,0:T(8,128)} %bitcast.63), custom_call_target="tpu_custom_call" | custom-call | flops 8589934592 | bytes 20971520 | tf_op jit(solution)/shard_map/bwd_first/pallas_call | solution.py:399
  190.5 25.6 %collective-permute-done.11 = bf16[512,2048]{1,0:T(8,128)(2,1)} collective-permute-done((bf16[512,2048]{1,0:T(8,128)(2,1)}, bf16[512,2048]{1,0:T(8,128)(2,1)}, u32[]{:S(2)}, u32[]{:S(2)}) %collective-permute-start.11) | collective-permute-done | bytes 2097184 | tf_op jit(solution)/shard_map/ppermute | solution.py:446
  218.8 20.8 %collective-permute-done.3 = bf16[512,2048]{1,0:T(8,128)(2,1)S(1)} collective-permute-done((bf16[512,2048]{1,0:T(8,128)(2,1)S(1)}, bf16[512,2048]{1,0:T(8,128)(2,1)S(1)}, u32[]{:S(2)}, u32[]{:S(2)}) %collective-permute-start.3) | collective-permute-done | bytes 2097184 | tf_op jit(solution)/shard_map/ppermute | solution.py:447
  241.6 19.5 %collective-permute-done.5 = bf16[512,2048]{1,0:T(8,128)(2,1)} collective-permute-done((bf16[512,2048]{1,0:T(8,128)(2,1)S(1)}, bf16[512,2048]{1,0:T(8,128)(2,1)}, u32[]{:S(2)}, u32[]{:S(2)}) %collective-permute-start.5) | collective-permute-done | bytes 2097184 | tf_op jit(solution)/shard_map/ppermute | solution.py:446
  267.4 17.1 %collective-permute-done.12 = bf16[2048,512]{1,0:T(8,128)(2,1)S(1)} collective-permute-done((bf16[2048,512]{1,0:T(8,128)(2,1)S(1)}, bf16[2048,512]{1,0:T(8,128)(2,1)S(1)}, u32[]{:S(2)}, u32[]{:S(2)}) %collective-permute-start.12) | collective-permute-done | bytes 2097184 | tf_op jit(solution)/shard_map/ppermute | solution.py:447
  440.9 22.2 %chain.4 = (bf16[1,1024,512]{2,1,0:T(8,128)(2,1)S(1)}, bf16[1024,2048]{1,0:T(8,128)(2,1)}, f32[1024,256]{1,0:T(8,128)S(1)}, f32[2048,256]{1,0:T(8,128)}, bf16[20...) custom-call(bf16[1,1024,512]{2,1,0:T(8,128)(2,1)S(1)} %bitcast.52, f32[1,512,2048]{2,1,0:T(8,128)} %fusion.9.refs_1_.w1_ref, ...), custom_call_target="tpu_custom_call" | custom-call | flops 8589934592 | bytes 22020096 | tf_op jit(solution)/shard_map/chain/pallas_call | solution.py:211
  464.0 18.0 %tail.4 = (f32[1024,256]{1,0:T(8,128)S(1)}, bf16[1024,2048]{1,0:T(8,128)(2,1)}, f32[512,2048]{1,0:T(8,128)}, bf16[512,2048]{1,0:T(8,128)(2,1)}, f32[2048,256]{1,0:T(8,128)}) custom-call(bf16[1024,2048]{1,0:T(8,128)(2,1)} %get-tuple-element.148.refs_0_.a_ref, bf16[1,1024,512]{2,1,0:T(8,128)(2,1)S(1)} %get-tuple-element.149.refs_1_.refs_2_.h_ref, ...), custom_call_target="tpu_custom_call" | custom-call | flops 7516192768 | bytes 23068672 | tf_op jit(solution)/shard_map/tail/pallas_call | solution.py:301
  497.1 55.1 %collective-permute-done.33 = bf16[2048,256]{1,0:T(8,128)(2,1)S(1)} collective-permute-done((bf16[2048,256]{1,0:T(8,128)(2,1)S(1)}, bf16[2048,256]{1,0:T(8,128)(2,1)S(1)}, u32[]{:S(2)}, u32[]{:S(2)}) %collective-permute-start.33) | collective-permute-done | bytes 1048608 | tf_op jit(solution)/shard_map/ppermute | solution.py:447
  554.6 20.2 %bwd_mid.8 = (f32[512,2048]{1,0:T(8,128)}, bf16[512,2048]{1,0:T(8,128)(2,1)S(1)}, f32[2048,512]{1,0:T(8,128)}, bf16[2048,512]{1,0:T(8,128)(2,1)S(1)}, f32[1024,512]{1,0:T(8,128)}) custom-call(f32[1024,512]{1,0:T(8,128)} %get-tuple-element.157.e_ref, bf16[1,1024,512]{2,1,0:T(8,128)(2,1)S(1)} %bitcast.53, f32[1,512,2048]{2,1,0:T(8,128)} %fusion.9.refs_1_.w1_ref, ...), custom_call_target="tpu_custom_call" | custom-call | flops 10737418240 | bytes 20971520 | tf_op jit(solution)/shard_map/bwd_mid/pallas_call | solution.py:399
  578.9 20.3 %bwd_mid.9 = (f32[512,2048]{1,0:T(8,128)}, bf16[512,2048]{1,0:T(8,128)(2,1)S(1)}, f32[2048,512]{1,0:T(8,128)}, bf16[2048,512]{1,0:T(8,128)(2,1)S(1)}, f32[1024,512]{1,0:T(8,128)}) custom-call(f32[1024,512]{1,0:T(8,128)} %get-tuple-element.159.e_ref, bf16[1,1024,512]{2,1,0:T(8,128)(2,1)S(1)} %bitcast.51, f32[1,512,2048]{2,1,0:T(8,128)} %fusion.5.w1_ref, ...), custom_call_target="tpu_custom_call" | custom-call | flops 10737418240 | bytes 20971520 | tf_op jit(solution)/shard_map/bwd_mid/pallas_call | solution.py:399
  599.3 16.7 %bwd_first.4 = (f32[512,2048]{1,0:T(8,128)}, bf16[512,2048]{1,0:T(8,128)(2,1)S(1)}, f32[2048,512]{1,0:T(8,128)}, bf16[2048,512]{1,0:T(8,128)(2,1)S(1)}) custom-call(f32[1024,512]{1,0:T(8,128)} %get-tuple-element.160.e_ref, bf16[3,1024,512]{2,1,0:T(8,128)(2,1)} %bitcast.44, f32[1,512,2048]{2,1,0:T(8,128)} %fusion.1.w1_ref, f32[1,2048,512]{2,1,0:T(8,128)} %fusion.3.w2_ref), custom_call_target="tpu_custom_call" | custom-call | flops 8589934592 | bytes 20971520 | tf_op jit(solution)/shard_map/bwd_first/pallas_call | solution.py:399
  623.7 22.7 %collective-permute-done.38 = bf16[512,2048]{1,0:T(8,128)(2,1)} collective-permute-done((bf16[512,2048]{1,0:T(8,128)(2,1)S(1)}, bf16[512,2048]{1,0:T(8,128)(2,1)}, u32[]{:S(2)}, u32[]{:S(2)}) %collective-permute-start.38) | collective-permute-done | bytes 2097184 | tf_op jit(solution)/shard_map/ppermute | solution.py:446
  649.0 19.2 %collective-permute-done.30 = bf16[512,2048]{1,0:T(8,128)(2,1)S(1)} collective-permute-done((bf16[512,2048]{1,0:T(8,128)(2,1)S(1)}, bf16[512,2048]{1,0:T(8,128)(2,1)S(1)}, u32[]{:S(2)}, u32[]{:S(2)}) %collective-permute-start.30) | collective-permute-done | bytes 2097184 | tf_op jit(solution)/shard_map/ppermute | solution.py:447
  668.5 22.7 %collective-permute-done.32 = bf16[512,2048]{1,0:T(8,128)(2,1)S(1)} collective-permute-done((bf16[512,2048]{1,0:T(8,128)(2,1)S(1)}, bf16[512,2048]{1,0:T(8,128)(2,1)S(1)}, u32[]{:S(2)}, u32[]{:S(2)}) %collective-permute-start.32) | collective-permute-done | bytes 2097184 | tf_op jit(solution)/shard_map/ppermute | solution.py:446
  719.7 16.5 %collective-permute-done.41 = bf16[2048,512]{1,0:T(8,128)(2,1)} collective-permute-done((bf16[2048,512]{1,0:T(8,128)(2,1)S(1)}, bf16[2048,512]{1,0:T(8,128)(2,1)}, u32[]{:S(2)}, u32[]{:S(2)}) %collective-permute-start.41) | collective-permute-done | bytes 2097184 | tf_op jit(solution)/shard_map/ppermute | solution.py:446
  762.1 19.1 %collective-permute-done.44 = bf16[512,2048]{1,0:T(8,128)(2,1)} collective-permute-done((bf16[512,2048]{1,0:T(8,128)(2,1)S(1)}, bf16[512,2048]{1,0:T(8,128)(2,1)}, u32[]{:S(2)}, u32[]{:S(2)}) %collective-permute-start.44) | collective-permute-done | bytes 2097184 | tf_op jit(solution)/shard_map/ppermute | solution.py:446
  871.1 22.1 %chain.5 = (bf16[1,1024,512]{2,1,0:T(8,128)(2,1)S(1)}, bf16[1024,2048]{1,0:T(8,128)(2,1)}, f32[1024,256]{1,0:T(8,128)S(1)}, f32[2048,256]{1,0:T(8,128)}, bf16[20...) custom-call(bf16[1,1024,512]{2,1,0:T(8,128)(2,1)S(1)} %bitcast.54, f32[1,512,2048]{2,1,0:T(8,128)} %fusion.21.refs_1_.w1_ref, ...), custom_call_target="tpu_custom_call" | custom-call | flops 8589934592 | bytes 22020096 | tf_op jit(solution)/shard_map/chain/pallas_call | solution.py:211
  894.2 17.8 %tail.5 = (f32[1024,256]{1,0:T(8,128)S(1)}, bf16[1024,2048]{1,0:T(8,128)(2,1)}, f32[512,2048]{1,0:T(8,128)}, bf16[512,2048]{1,0:T(8,128)(2,1)}, f32[2048,256]{1,0:T(8,128)}) custom-call(bf16[1024,2048]{1,0:T(8,128)(2,1)} %get-tuple-element.183.refs_0_.a_ref, bf16[1,1024,512]{2,1,0:T(8,128)(2,1)S(1)} %get-tuple-element.184.refs_1_.refs_2_.h_ref, ...), custom_call_target="tpu_custom_call" | custom-call | flops 7516192768 | bytes 23068672 | tf_op jit(solution)/shard_map/tail/pallas_call | solution.py:301
  928.4 54.4 %collective-permute-done.54.prev_ref = bf16[2048,256]{1,0:T(8,128)(2,1)S(1)} collective-permute-done((bf16[2048,256]{1,0:T(8,128)(2,1)S(1)}, bf16[2048,256]{1,0:T(8,128)(2,1)S(1)}, u32[]{:S(2)}, u32[]{:S(2)}) %collective-permute-start.54) | collective-permute-done | bytes 1048608 | tf_op jit(solution)/shard_map/ppermute | solution.py:447
  986.1 20.4 %bwd_mid.10 = (f32[512,2048]{1,0:T(8,128)}, bf16[512,2048]{1,0:T(8,128)(2,1)}, f32[2048,512]{1,0:T(8,128)}, bf16[2048,512]{1,0:T(8,128)(2,1)S(1)}, f32[1024,512]{1,0:T(8,128)}) custom-call(f32[1024,512]{1,0:T(8,128)} %get-tuple-element.193.e_ref, bf16[1,1024,512]{2,1,0:T(8,128)(2,1)S(1)} %bitcast.55, f32[1,512,2048]{2,1,0:T(8,128)} %fusion.21.refs_1_.w1_ref, ...), custom_call_target="tpu_custom_call" | custom-call | flops 10737418240 | bytes 20971520 | tf_op jit(solution)/shard_map/bwd_mid/pallas_call | solution.py:399
  1011.3 20.5 %bwd_mid.11 = (f32[512,2048]{1,0:T(8,128)}, bf16[512,2048]{1,0:T(8,128)(2,1)S(1)}, f32[2048,512]{1,0:T(8,128)}, bf16[2048,512]{1,0:T(8,128)(2,1)S(1)}, f32[1024,512]{1,0:T(8,128)}) custom-call(f32[1024,512]{1,0:T(8,128)} %get-tuple-element.195.e_ref, bf16[1,1024,512]{2,1,0:T(8,128)(2,1)S(1)} %bitcast.49, f32[1,512,2048]{2,1,0:T(8,128)} %fusion.17.w1_ref, ...), custom_call_target="tpu_custom_call" | custom-call | flops 10737418240 | bytes 20971520 | tf_op jit(solution)/shard_map/bwd_mid/pallas_call | solution.py:399
  1034.3 16.3 %bwd_first.5 = (f32[512,2048]{1,0:T(8,128)}, bf16[512,2048]{1,0:T(8,128)(2,1)}, f32[2048,512]{1,0:T(8,128)}, bf16[2048,512]{1,0:T(8,128)(2,1)S(1)}) custom-call(f32[1024,512]{1,0:T(8,128)} %get-tuple-element.197.e_ref, bf16[3,1024,512]{2,1,0:T(8,128)(2,1)} %bitcast.45, f32[1,512,2048]{2,1,0:T(8,128)} %fusion.13.w1_ref, f32[1,2048,512]{2,1,0:T(8,128)} %fusion.15.w2_ref), custom_call_target="tpu_custom_call" | custom-call | flops 8589934592 | bytes 20971520 | tf_op jit(solution)/shard_map/bwd_first/pallas_call | solution.py:399
  1084.8 20.5 %collective-permute-done.66.prev_ref = bf16[512,2048]{1,0:T(8,128)(2,1)S(1)} collective-permute-done((bf16[512,2048]{1,0:T(8,128)(2,1)}, bf16[512,2048]{1,0:T(8,128)(2,1)S(1)}, u32[]{:S(2)}, u32[]{:S(2)}) %collective-permute-start.66) | collective-permute-done | bytes 2097184 | tf_op jit(solution)/shard_map/ppermute | solution.py:447
  1129.9 20.3 %collective-permute-done.63.prev_ref = bf16[2048,512]{1,0:T(8,128)(2,1)S(1)} collective-permute-done((bf16[2048,512]{1,0:T(8,128)(2,1)S(1)}, bf16[2048,512]{1,0:T(8,128)(2,1)S(1)}, u32[]{:S(2)}, u32[]{:S(2)}) %collective-permute-start.63) | collective-permute-done | bytes 2097184 | tf_op jit(solution)/shard_map/ppermute | solution.py:447
  1174.8 20.3 %collective-permute-done.72.prev_ref = bf16[512,2048]{1,0:T(8,128)(2,1)S(1)} collective-permute-done((bf16[512,2048]{1,0:T(8,128)(2,1)S(1)}, bf16[512,2048]{1,0:T(8,128)(2,1)S(1)}, u32[]{:S(2)}, u32[]{:S(2)}) %collective-permute-start.72) | collective-permute-done | bytes 2097184 | tf_op jit(solution)/shard_map/ppermute | solution.py:447
  1220.9 19.1 %collective-permute-done.69.prev_ref = bf16[2048,512]{1,0:T(8,128)(2,1)S(1)} collective-permute-done((bf16[2048,512]{1,0:T(8,128)(2,1)S(1)}, bf16[2048,512]{1,0:T(8,128)(2,1)S(1)}, u32[]{:S(2)}, u32[]{:S(2)}) %collective-permute-start.69) | collective-permute-done | bytes 2097184 | tf_op jit(solution)/shard_map/ppermute | solution.py:447
  1264.6 20.4 %collective-permute-done.78.prev_ref = bf16[2048,512]{1,0:T(8,128)(2,1)S(1)} collective-permute-done((bf16[2048,512]{1,0:T(8,128)(2,1)S(1)}, bf16[2048,512]{1,0:T(8,128)(2,1)S(1)}, u32[]{:S(2)}, u32[]{:S(2)}) %collective-permute-start.78) | collective-permute-done | bytes 2097184 | tf_op jit(solution)/shard_map/ppermute | solution.py:447
  (285 shorter events, 571.1 us)
Async XLA Ops:
  51.9 93.7 %collective-permute-start = (bf16[512,2048]{1,0:T(8,128)(2,1)S(1)}, bf16[512,2048]{1,0:T(8,128)(2,1)S(1)}, u32[]{:S(2)}, u32[]{:S(2)}) collective-permute-start(bf16[512,2048]{1,0:T(8,128)(2,1)S(1)} %get-tuple-element.128), channel_id=1, source_target_pairs={{0,1},{1,2},{2,3},{3,4},{4,5},{5,6},{6,7},{7,0},{8,9},{9,10},{10,1... | collective-permute-start | bytes 6291464 | tf_op jit(solution)/shard_map/ppermute | solution.py:447
  52.6 68.9 %collective-permute-start.6 = (bf16[2048,256]{1,0:T(8,128)(2,1)S(1)}, bf16[2048,256]{1,0:T(8,128)(2,1)S(1)}, u32[]{:S(2)}, u32[]{:S(2)}) collective-permute-start(bf16[2048,256]{1,0:T(8,128)(2,1)S(1)} %get-tuple-element.133), channel_id=1, source_target_pairs={{0,1},{1,2},{2,3},{3,4},{4,5},{5,6},{6,7},{7,0},{8,9},{9,10},{10,1... | collective-permute-start | bytes 3145736 | tf_op jit(solution)/shard_map/ppermute | solution.py:447
  55.3 90.2 %collective-permute-start.7 = (bf16[2048,256]{1,0:T(8,128)(2,1)S(1)}, bf16[2048,256]{1,0:T(8,128)(2,1)}, u32[]{:S(2)}, u32[]{:S(2)}) collective-permute-start(bf16[2048,256]{1,0:T(8,128)(2,1)S(1)} %get-tuple-element.133), channel_id=1, source_target_pairs={{0,7},{1,0},{2,1},{3,2},{4,3},{5,4},{6,5},{7,6},{8,15},{9,8},{10,9... | collective-permute-start | bytes 3145736 | tf_op jit(solution)/shard_map/ppermute | solution.py:448
  55.6 89.8 %collective-permute-start.8 = (bf16[2048,256]{1,0:T(8,128)(2,1)S(1)}, bf16[2048,256]{1,0:T(8,128)(2,1)}, u32[]{:S(2)}, u32[]{:S(2)}) collective-permute-start(bf16[2048,256]{1,0:T(8,128)(2,1)S(1)} %get-tuple-element.133), channel_id=1, source_target_pairs={{0,8},{8,0},{1,9},{9,1},{2,10},{10,2},{3,11},{11,3},{4,12},{12,4},... | collective-permute-start | bytes 3145736 | tf_op jit(solution)/shard_map/ppermute | solution.py:446
  57.9 125.7 %collective-permute-start.1 = (bf16[512,2048]{1,0:T(8,128)(2,1)S(1)}, bf16[512,2048]{1,0:T(8,128)(2,1)}, u32[]{:S(2)}, u32[]{:S(2)}) collective-permute-start(bf16[512,2048]{1,0:T(8,128)(2,1)S(1)} %get-tuple-element.128), channel_id=1, source_target_pairs={{0,7},{1,0},{2,1},{3,2},{4,3},{5,4},{6,5},{7,6},{8,15},{9,8},{10,9... | collective-permute-start | bytes 6291464 | tf_op jit(solution)/shard_map/ppermute | solution.py:448
  145.5 70.6 %collective-permute-start.11 = (bf16[512,2048]{1,0:T(8,128)(2,1)}, bf16[512,2048]{1,0:T(8,128)(2,1)}, u32[]{:S(2)}, u32[]{:S(2)}) collective-permute-start(bf16[512,2048]{1,0:T(8,128)(2,1)} %get-tuple-element.134), channel_id=1, source_target_pairs={{0,8},{8,0},{1,9},{9,1},{2,10},{10,2},{3,11},{11,3},{4,12},{12,4},... | collective-permute-start | bytes 6291464 | tf_op jit(solution)/shard_map/ppermute | solution.py:446
  145.6 70.6 %collective-permute-start.9 = (bf16[512,2048]{1,0:T(8,128)(2,1)}, bf16[512,2048]{1,0:T(8,128)(2,1)}, u32[]{:S(2)}, u32[]{:S(2)}) collective-permute-start(bf16[512,2048]{1,0:T(8,128)(2,1)} %get-tuple-element.134), channel_id=1, source_target_pairs={{0,1},{1,2},{2,3},{3,4},{4,5},{5,6},{6,7},{7,0},{8,9},{9,10},{10,1... | collective-permute-start | bytes 6291464 | tf_op jit(solution)/shard_map/ppermute | solution.py:447
  190.5 70.6 %collective-permute-start.5 = (bf16[512,2048]{1,0:T(8,128)(2,1)S(1)}, bf16[512,2048]{1,0:T(8,128)(2,1)}, u32[]{:S(2)}, u32[]{:S(2)}) collective-permute-start(bf16[512,2048]{1,0:T(8,128)(2,1)S(1)} %get-tuple-element.129), channel_id=1, source_target_pairs={{0,8},{8,0},{1,9},{9,1},{2,10},{10,2},{3,11},{11,3},{4,12},{12,4},... | collective-permute-start | bytes 6291464 | tf_op jit(solution)/shard_map/ppermute | solution.py:446
  216.1 76.3 %collective-permute-start.13 = (bf16[2048,512]{1,0:T(8,128)(2,1)S(1)}, bf16[2048,512]{1,0:T(8,128)(2,1)}, u32[]{:S(2)}, u32[]{:S(2)}) collective-permute-start(bf16[2048,512]{1,0:T(8,128)(2,1)S(1)} %get-tuple-element.135), channel_id=1, source_target_pairs={{0,7},{1,0},{2,1},{3,2},{4,3},{5,4},{6,5},{7,6},{8,15},{9,8},{10,9... | collective-permute-start | bytes 6291464 | tf_op jit(solution)/shard_map/ppermute | solution.py:448
  261.1 68.5 %collective-permute-start.15 = (bf16[512,2048]{1,0:T(8,128)(2,1)S(1)}, bf16[512,2048]{1,0:T(8,128)(2,1)}, u32[]{:S(2)}, u32[]{:S(2)}) collective-permute-start(bf16[512,2048]{1,0:T(8,128)(2,1)S(1)} %get-tuple-element.138), channel_id=1, source_target_pairs={{0,1},{1,2},{2,3},{3,4},{4,5},{5,6},{6,7},{7,0},{8,9},{9,10},{10,1... | collective-permute-start | bytes 6291464 | tf_op jit(solution)/shard_map/ppermute | solution.py:447
  264.8 72.1 %collective-permute-start.16 = (bf16[512,2048]{1,0:T(8,128)(2,1)S(1)}, bf16[512,2048]{1,0:T(8,128)(2,1)}, u32[]{:S(2)}, u32[]{:S(2)}) collective-permute-start(bf16[512,2048]{1,0:T(8,128)(2,1)S(1)} %get-tuple-element.138), channel_id=1, source_target_pairs={{0,7},{1,0},{2,1},{3,2},{4,3},{5,4},{6,5},{7,6},{8,15},{9,8},{10,9... | collective-permute-start | bytes 6291464 | tf_op jit(solution)/shard_map/ppermute | solution.py:448
  306.0 68.5 %collective-permute-start.18 = (bf16[2048,512]{1,0:T(8,128)(2,1)S(1)}, bf16[2048,512]{1,0:T(8,128)(2,1)}, u32[]{:S(2)}, u32[]{:S(2)}) collective-permute-start(bf16[2048,512]{1,0:T(8,128)(2,1)S(1)} %get-tuple-element.141), channel_id=1, source_target_pairs={{0,1},{1,2},{2,3},{3,4},{4,5},{5,6},{6,7},{7,0},{8,9},{9,10},{10,1... | collective-permute-start | bytes 6291464 | tf_op jit(solution)/shard_map/ppermute | solution.py:447
  312.7 80.0 %collective-permute-start.19 = (bf16[2048,512]{1,0:T(8,128)(2,1)S(1)}, bf16[2048,512]{1,0:T(8,128)(2,1)}, u32[]{:S(2)}, u32[]{:S(2)}) collective-permute-start(bf16[2048,512]{1,0:T(8,128)(2,1)S(1)} %get-tuple-element.141), channel_id=1, source_target_pairs={{0,7},{1,0},{2,1},{3,2},{4,3},{5,4},{6,5},{7,6},{8,15},{9,8},{10,9... | collective-permute-start | bytes 6291464 | tf_op jit(solution)/shard_map/ppermute | solution.py:448
  356.7 72.9 %collective-permute-start.22 = (bf16[2048,512]{1,0:T(8,128)(2,1)S(1)}, bf16[2048,512]{1,0:T(8,128)(2,1)S(1)}, u32[]{:S(2)}, u32[]{:S(2)}) collective-permute-start(bf16[2048,512]{1,0:T(8,128)(2,1)S(1)} %get-tuple-element.145), channel_id=1, source_target_pairs={{0,7},{1,0},{2,1},{3,2},{4,3},{5,4},{6,5},{7,6},{8,15},{9,8},{10,9... | collective-permute-start | bytes 6291464 | tf_op jit(solution)/shard_map/ppermute | solution.py:448
  482.0 95.5 %collective-permute-start.27 = (bf16[512,2048]{1,0:T(8,128)(2,1)}, bf16[512,2048]{1,0:T(8,128)(2,1)S(1)}, u32[]{:S(2)}, u32[]{:S(2)}) collective-permute-start(bf16[512,2048]{1,0:T(8,128)(2,1)} %get-tuple-element.163), channel_id=1, source_target_pairs={{0,1},{1,2},{2,3},{3,4},{4,5},{5,6},{6,7},{7,0},{8,9},{9,10},{10,1... | collective-permute-start | bytes 6291464 | tf_op jit(solution)/shard_map/ppermute | solution.py:447
  482.0 70.2 %collective-permute-start.33 = (bf16[2048,256]{1,0:T(8,128)(2,1)S(1)}, bf16[2048,256]{1,0:T(8,128)(2,1)S(1)}, u32[]{:S(2)}, u32[]{:S(2)}) collective-permute-start(bf16[2048,256]{1,0:T(8,128)(2,1)S(1)} %get-tuple-element.168), channel_id=1, source_target_pairs={{0,1},{1,2},{2,3},{3,4},{4,5},{5,6},{6,7},{7,0},{8,9},{9,10},{10,1... | collective-permute-start | bytes 3145736 | tf_op jit(solution)/shard_map/ppermute | solution.py:447
  484.0 90.8 %collective-permute-start.34 = (bf16[2048,256]{1,0:T(8,128)(2,1)S(1)}, bf16[2048,256]{1,0:T(8,128)(2,1)S(1)}, u32[]{:S(2)}, u32[]{:S(2)}) collective-permute-start(bf16[2048,256]{1,0:T(8,128)(2,1)S(1)} %get-tuple-element.168), channel_id=1, source_target_pairs={{0,7},{1,0},{2,1},{3,2},{4,3},{5,4},{6,5},{7,6},{8,15},{9,8},{10,9... | collective-permute-start | bytes 3145736 | tf_op jit(solution)/shard_map/ppermute | solution.py:448
  484.7 90.1 %collective-permute-start.35 = (bf16[2048,256]{1,0:T(8,128)(2,1)S(1)}, bf16[2048,256]{1,0:T(8,128)(2,1)S(1)}, u32[]{:S(2)}, u32[]{:S(2)}) collective-permute-start(bf16[2048,256]{1,0:T(8,128)(2,1)S(1)} %get-tuple-element.168), channel_id=1, source_target_pairs={{0,8},{8,0},{1,9},{9,1},{2,10},{10,2},{3,11},{11,3},{4,12},{12,4},... | collective-permute-start | bytes 3145736 | tf_op jit(solution)/shard_map/ppermute | solution.py:446
  486.7 129.3 %collective-permute-start.28 = (bf16[512,2048]{1,0:T(8,128)(2,1)}, bf16[512,2048]{1,0:T(8,128)(2,1)}, u32[]{:S(2)}, u32[]{:S(2)}) collective-permute-start(bf16[512,2048]{1,0:T(8,128)(2,1)} %get-tuple-element.163), channel_id=1, source_target_pairs={{0,7},{1,0},{2,1},{3,2},{4,3},{5,4},{6,5},{7,6},{8,15},{9,8},{10,9... | collective-permute-start | bytes 6291464 | tf_op jit(solution)/shard_map/ppermute | solution.py:448
  577.5 68.8 %collective-permute-start.38 = (bf16[512,2048]{1,0:T(8,128)(2,1)S(1)}, bf16[512,2048]{1,0:T(8,128)(2,1)}, u32[]{:S(2)}, u32[]{:S(2)}) collective-permute-start(bf16[512,2048]{1,0:T(8,128)(2,1)S(1)} %get-tuple-element.169), channel_id=1, source_target_pairs={{0,8},{8,0},{1,9},{9,1},{2,10},{10,2},{3,11},{11,3},{4,12},{12,4},... | collective-permute-start | bytes 6291464 | tf_op jit(solution)/shard_map/ppermute | solution.py:446
  646.4 73.3 %collective-permute-start.40 = (bf16[2048,512]{1,0:T(8,128)(2,1)S(1)}, bf16[2048,512]{1,0:T(8,128)(2,1)}, u32[]{:S(2)}, u32[]{:S(2)}) collective-permute-start(bf16[2048,512]{1,0:T(8,128)(2,1)S(1)} %get-tuple-element.170), channel_id=1, source_target_pairs={{0,7},{1,0},{2,1},{3,2},{4,3},{5,4},{6,5},{7,6},{8,15},{9,8},{10,9... | collective-permute-start | bytes 6291464 | tf_op jit(solution)/shard_map/ppermute | solution.py:448
  742.9 77.2 %collective-permute-start.46 = (bf16[2048,512]{1,0:T(8,128)(2,1)S(1)}, bf16[2048,512]{1,0:T(8,128)(2,1)}, u32[]{:S(2)}, u32[]{:S(2)}) collective-permute-start(bf16[2048,512]{1,0:T(8,128)(2,1)S(1)} %get-tuple-element.176), channel_id=1, source_target_pairs={{0,7},{1,0},{2,1},{3,2},{4,3},{5,4},{6,5},{7,6},{8,15},{9,8},{10,9... | collective-permute-start | bytes 6291464 | tf_op jit(solution)/shard_map/ppermute | solution.py:448
  786.9 70.2 %collective-permute-start.49 = (bf16[2048,512]{1,0:T(8,128)(2,1)S(1)}, bf16[2048,512]{1,0:T(8,128)(2,1)}, u32[]{:S(2)}, u32[]{:S(2)}) collective-permute-start(bf16[2048,512]{1,0:T(8,128)(2,1)S(1)} %get-tuple-element.180), channel_id=1, source_target_pairs={{0,7},{1,0},{2,1},{3,2},{4,3},{5,4},{6,5},{7,6},{8,15},{9,8},{10,9... | collective-permute-start | bytes 6291464 | tf_op jit(solution)/shard_map/ppermute | solution.py:448
  912.0 99.2 %collective-permute-start.60 = (bf16[512,2048]{1,0:T(8,128)(2,1)}, bf16[512,2048]{1,0:T(8,128)(2,1)S(1)}, u32[]{:S(2)}, u32[]{:S(2)}) collective-permute-start(bf16[512,2048]{1,0:T(8,128)(2,1)} %get-tuple-element.205), channel_id=1, source_target_pairs={{0,1},{1,2},{2,3},{3,4},{4,5},{5,6},{6,7},{7,0},{8,9},{9,10},{10,1... | collective-permute-start | bytes 6291464 | tf_op jit(solution)/shard_map/ppermute | solution.py:447
  912.0 70.8 %collective-permute-start.54 = (bf16[2048,256]{1,0:T(8,128)(2,1)S(1)}, bf16[2048,256]{1,0:T(8,128)(2,1)S(1)}, u32[]{:S(2)}, u32[]{:S(2)}) collective-permute-start(bf16[2048,256]{1,0:T(8,128)(2,1)S(1)} %get-tuple-element.200), channel_id=1, source_target_pairs={{0,1},{1,2},{2,3},{3,4},{4,5},{5,6},{6,7},{7,0},{8,9},{9,10},{10,1... | collective-permute-start | bytes 3145736 | tf_op jit(solution)/shard_map/ppermute | solution.py:447
  913.0 137.6 %collective-permute-start.61 = (bf16[512,2048]{1,0:T(8,128)(2,1)}, bf16[512,2048]{1,0:T(8,128)(2,1)S(1)}, u32[]{:S(2)}, u32[]{:S(2)}) collective-permute-start(bf16[512,2048]{1,0:T(8,128)(2,1)} %get-tuple-element.205), channel_id=1, source_target_pairs={{0,7},{1,0},{2,1},{3,2},{4,3},{5,4},{6,5},{7,6},{8,15},{9,8},{10,9... | collective-permute-start | bytes 6291464 | tf_op jit(solution)/shard_map/ppermute | solution.py:448
  914.7 91.8 %collective-permute-start.55 = (bf16[2048,256]{1,0:T(8,128)(2,1)S(1)}, bf16[2048,256]{1,0:T(8,128)(2,1)S(1)}, u32[]{:S(2)}, u32[]{:S(2)}) collective-permute-start(bf16[2048,256]{1,0:T(8,128)(2,1)S(1)} %get-tuple-element.200), channel_id=1, source_target_pairs={{0,7},{1,0},{2,1},{3,2},{4,3},{5,4},{6,5},{7,6},{8,15},{9,8},{10,9... | collective-permute-start | bytes 3145736 | tf_op jit(solution)/shard_map/ppermute | solution.py:448
  915.2 91.3 %collective-permute-start.56 = (bf16[2048,256]{1,0:T(8,128)(2,1)S(1)}, bf16[2048,256]{1,0:T(8,128)(2,1)S(1)}, u32[]{:S(2)}, u32[]{:S(2)}) collective-permute-start(bf16[2048,256]{1,0:T(8,128)(2,1)S(1)} %get-tuple-element.200), channel_id=1, source_target_pairs={{0,8},{8,0},{1,9},{9,1},{2,10},{10,2},{3,11},{11,3},{4,12},{12,4},... | collective-permute-start | bytes 3145736 | tf_op jit(solution)/shard_map/ppermute | solution.py:446
  1082.1 70.1 %collective-permute-start.64 = (bf16[2048,512]{1,0:T(8,128)(2,1)S(1)}, bf16[2048,512]{1,0:T(8,128)(2,1)S(1)}, u32[]{:S(2)}, u32[]{:S(2)}) collective-permute-start(bf16[2048,512]{1,0:T(8,128)(2,1)S(1)} %get-tuple-element.210), channel_id=1, source_target_pairs={{0,7},{1,0},{2,1},{3,2},{4,3},{5,4},{6,5},{7,6},{8,15},{9,8},{10,9... | collective-permute-start | bytes 6291464 | tf_op jit(solution)/shard_map/ppermute | solution.py:448
  1127.2 69.9 %collective-permute-start.73 = (bf16[512,2048]{1,0:T(8,128)(2,1)S(1)}, bf16[512,2048]{1,0:T(8,128)(2,1)S(1)}, u32[]{:S(2)}, u32[]{:S(2)}) collective-permute-start(bf16[512,2048]{1,0:T(8,128)(2,1)S(1)} %copy-done.10), channel_id=1, source_target_pairs={{0,7},{1,0},{2,1},{3,2},{4,3},{5,4},{6,5},{7,6},{8,15},{9,8},{10,9... | collective-permute-start | bytes 6291464 | tf_op jit(solution)/shard_map/ppermute | solution.py:448
  1172.2 69.9 %collective-permute-start.70 = (bf16[2048,512]{1,0:T(8,128)(2,1)S(1)}, bf16[2048,512]{1,0:T(8,128)(2,1)S(1)}, u32[]{:S(2)}, u32[]{:S(2)}) collective-permute-start(bf16[2048,512]{1,0:T(8,128)(2,1)S(1)} %copy-done.8), channel_id=1, source_target_pairs={{0,7},{1,0},{2,1},{3,2},{4,3},{5,4},{6,5},{7,6},{8,15},{9,8},{10,9... | collective-permute-start | bytes 6291464 | tf_op jit(solution)/shard_map/ppermute | solution.py:448
  1218.3 68.7 %collective-permute-start.79 = (bf16[2048,512]{1,0:T(8,128)(2,1)S(1)}, bf16[2048,512]{1,0:T(8,128)(2,1)S(1)}, u32[]{:S(2)}, u32[]{:S(2)}) collective-permute-start(bf16[2048,512]{1,0:T(8,128)(2,1)S(1)} %copy-done.6), channel_id=1, source_target_pairs={{0,7},{1,0},{2,1},{3,2},{4,3},{5,4},{6,5},{7,6},{8,15},{9,8},{10,9... | collective-permute-start | bytes 6291464 | tf_op jit(solution)/shard_map/ppermute | solution.py:448
  (104 other events, 4210.1 us)
where the time goes:
time: 1330 us; the launch traced here: 1320 us
  waiting for transfers between devices  712 us (54%)
  Pallas kernels  411 us (31%)
  starting transfers between devices  101 us (8%)
  other arithmetic  81.1 us (6%)
  local copies, waits for them, and re-layouts  14.3 us (1%)
    ppermute x27, waiting for transfers between devices, send(): prev = lax.ppermute(wire, 'col', from_col_prev)  422 us
    ppermute x27, waiting for transfers between devices, send(): row = lax.ppermute(wire, 'row', from_row)  286 us
    pallas_call x9, Pallas kernels, bwd_layer(): pl.pallas_call(functools.partial(bwd_body, with_next), grid=(f // TILE,),...  172 us
    broadcast_in_dim x14, other arithmetic, device_fn(): mix_vals(*vals)[None]  81.1 us
    pallas_call x3, Pallas kernels, chain(): pl.pallas_call(functools.partial(chain_body, n_fwd, nt, mixing, loss_scal...  78.5 us
    ppermute x27, starting transfers between devices, send(): nxt = lax.ppermute(wire, 'col', from_col_next)  55.7 us
    pallas_call x3, Pallas kernels, tail(): pl.pallas_call(functools.partial(tail_body, nt, mixing, loss_scale), grid...  52.9 us
    pallas_call x9, Pallas kernels, place(): pl.pallas_call(functools.partial(place_body, len(aliases)), grid=(4,), in...  43.4 us
  transfers between devices with their start and end apart: 81, of which 39 were waited for; matrix products, arithmetic and copies ran while one was open for 6% of the time, Pallas kernels for 24%

commit v1 on v0

--- a/solution.py
+++ b/solution.py
@@ -14,6 +14,7 @@
 GELU_K = 0.044715
 TILE = 512
 ROWS = 1024
+THIN = 128
 F32 = jnp.float32
 BF16 = jnp.bfloat16
 
@@ -51,11 +52,11 @@
     return inv * (m - n * jnp.mean(m * n, axis=-1, keepdims=True))
 
 
-def row_blocks(n):
-    return [slice(k, k + ROWS) for k in range(0, n, ROWS)]
-
-
-def params(mib=48):
+def row_blocks(n, rows=ROWS):
+    return [slice(k, k + rows) for k in range(0, n, rows)]
+
+
+def params(mib=62):
     return pltpu.CompilerParams(dimension_semantics=('arbitrary',), vmem_limit_bytes=mib << 20)
 
 
@@ -66,13 +67,14 @@
 def fwd_body(h_ref, w1_ref, w2_ref, hn_ref, n_scr, acc_scr):
     j = pl.program_id(0)
     blocks = row_blocks(h_ref.shape[0])
+    thin = row_blocks(h_ref.shape[0], THIN)
 
     @pl.when(j == 0)
     def _():
-        for r in blocks:
+        for r in thin:
             x = h_ref[r, :].astype(F32)
             n_scr[r, :] = (x * inv_rms_of(x)).astype(BF16)
-            acc_scr[r, :] = jnp.zeros((ROWS, acc_scr.shape[1]), F32)
+        acc_scr[...] = jnp.zeros_like(acc_scr)
 
     w1 = w1_ref[...].astype(BF16)
     w2 = w2_ref[...].astype(BF16)
@@ -82,7 +84,7 @@
 
     @pl.when(j == pl.num_programs(0) - 1)
     def _():
-        for r in blocks:
+        for r in thin:
             hn_ref[r, :] = (h_ref[r, :].astype(F32) + acc_scr[r, :]).astype(BF16)
 
 
@@ -102,7 +104,7 @@
     refs = list(refs)
     h_ref, hist_ref = refs.pop(0), None
     w1f_ref = refs.pop(0)
-    w2f_refs = [refs.pop(0) for _ in range(4 if mixing else 1)]
+    w2f_refs = [refs.pop(0) for _ in range(5 if mixing else 1)]
     t_ref, w1h_ref, w2h_ref = [refs.pop(0) for _ in range(3)]
     hist_ref, a_ref, e_ref, q_ref, wire_ref = [refs.pop(0) for _ in range(5)]
     if mixing:
@@ -115,6 +117,7 @@
     b = h_ref.shape[0]
     half = e_ref.shape[1]
     blocks = row_blocks(b)
+    thin = row_blocks(b, THIN)
 
     @pl.when(i == 0)
     def _():
@@ -122,7 +125,7 @@
 
     @pl.when((j == 0) & (i <= n_fwd * nt))
     def _():
-        for r in blocks:
+        for r in thin:
             x = h_scr[r, :].astype(F32)
             n_scr[r, :] = (x * inv_rms_of(x)).astype(BF16)
         acc_scr[...] = jnp.zeros_like(acc_scr)
@@ -131,7 +134,7 @@
     def _():
         w1 = w1f_ref[...].astype(BF16)
         if mixing:
-            w2 = mix_vals(*[w[...] for w in w2f_refs])
+            w2 = mix_refs(w2f_refs)
             p_ref[...] = w2
         else:
             w2 = w2f_refs[0][...]
@@ -142,7 +145,7 @@
 
     @pl.when(in_fwd & (j == nt - 1))
     def _():
-        for r in blocks:
+        for r in thin:
             out = (h_scr[r, :].astype(F32) + acc_scr[r, :]).astype(BF16)
             h_scr[r, :] = out
             hist_ref[r, :] = out
@@ -161,7 +164,7 @@
 
     @pl.when(in_head & (j == nt - 1))
     def _():
-        for r in blocks:
+        for r in thin:
             out = (h_scr[r, :half].astype(F32) + acc_scr[r, :half]).astype(BF16)
             e = loss_scale * (out.astype(F32) - t_ref[r, :].astype(F32))
             e_ref[r, :] = e
@@ -174,10 +177,10 @@
         wire_ref[...] = q.astype(BF16)
 
 
-def chain(n_fwd, h, hk, target, tk, w1f, k1f, w2f, k2f, w1h, k1h, w2h, k2h, half, loss_scale):
+def chain(n_fwd, h, hk, target, tk, w1f, k1f, w2f, k2f, w1h, k1h, w2h, k2h, half, loss_scale, even, tile):
     b, d = h.shape[1:]
     f = w1f.shape[2]
-    nt = f // TILE
+    nt = f // tile
     mixing = isinstance(w2f, tuple)
     n_steps = n_fwd * nt
 
@@ -194,34 +197,34 @@
         return jnp.maximum(i - n_steps - nt, 0)
 
     in_specs = [pl.BlockSpec((None, b, d), lambda i: (hk, 0, 0)),
-                pl.BlockSpec((None, d, TILE), lambda i: (k1f + f_layer(i), 0, f_tile(i)))]
+                pl.BlockSpec((None, d, tile), lambda i: (k1f + f_layer(i), 0, f_tile(i)))]
     if mixing:
-        in_specs += [pl.BlockSpec((TILE, d), lambda i: (f_tile(i), 0))] * 4
+        in_specs += [pl.BlockSpec((tile, d), lambda i: (f_tile(i), 0))] * 4 + [pl.BlockSpec(memory_space=pltpu.SMEM)]
     else:
-        in_specs.append(pl.BlockSpec((None, TILE, d), lambda i: (k2f + f_layer(i), f_tile(i), 0)))
-    in_specs += [pl.BlockSpec((None, b, half), lambda i: (tk, 0, 0)), pl.BlockSpec((None, d, TILE), lambda i: (k1h, 0, h_tile(i))),
-                 pl.BlockSpec((None, TILE, half), lambda i: (k2h, h_tile(i), 0))]
-    out_specs = [pl.BlockSpec((None, b, d), lambda i: (f_layer(i), 0, 0)), pl.BlockSpec((b, TILE), lambda i: (0, h_tile(i))),
-                 pl.BlockSpec((b, half), lambda i: (0, 0))] + [pl.BlockSpec((TILE, half), lambda i: (g_tile(i), 0))] * 2
+        in_specs.append(pl.BlockSpec((None, tile, d), lambda i: (k2f + f_layer(i), f_tile(i), 0)))
+    in_specs += [pl.BlockSpec((None, b, half), lambda i: (tk, 0, 0)), pl.BlockSpec((None, d, tile), lambda i: (k1h, 0, h_tile(i))),
+                 pl.BlockSpec((None, tile, half), lambda i: (k2h, h_tile(i), 0))]
+    out_specs = [pl.BlockSpec((None, b, d), lambda i: (f_layer(i), 0, 0)), pl.BlockSpec((b, tile), lambda i: (0, h_tile(i))),
+                 pl.BlockSpec((b, half), lambda i: (0, 0))] + [pl.BlockSpec((tile, half), lambda i: (g_tile(i), 0))] * 2
     out_shape = [jax.ShapeDtypeStruct((n_fwd, b, d), BF16), jax.ShapeDtypeStruct((b, f), BF16), jax.ShapeDtypeStruct((b, half), F32),
                  jax.ShapeDtypeStruct((f, half), F32), jax.ShapeDtypeStruct((f, half), BF16)]
     if mixing:
-        out_specs.append(pl.BlockSpec((TILE, d), lambda i: (f_tile(i), 0)))
+        out_specs.append(pl.BlockSpec((tile, d), lambda i: (f_tile(i), 0)))
         out_shape.append(jax.ShapeDtypeStruct((f, d), F32))
     return pl.pallas_call(
         functools.partial(chain_body, n_fwd, nt, mixing, loss_scale), grid=((n_fwd + 2) * nt,), name='chain',
         in_specs=in_specs, out_specs=out_specs, out_shape=out_shape,
-        scratch_shapes=[pltpu.VMEM((b, d), BF16), pltpu.VMEM((b, d), BF16), pltpu.VMEM((b, d), F32), pltpu.VMEM((nt, b, TILE), BF16),
-                        pltpu.VMEM((nt, TILE, half), F32), pltpu.VMEM((b, half), BF16)],
+        scratch_shapes=[pltpu.VMEM((b, d), BF16), pltpu.VMEM((b, d), BF16), pltpu.VMEM((b, d), F32), pltpu.VMEM((nt, b, tile), BF16),
+                        pltpu.VMEM((nt, tile, half), F32), pltpu.VMEM((b, half), BF16)],
         compiler_params=params(),
         cost_estimate=cost(2 * b * f * (2 * n_fwd * d + d + 2 * half), 8 * n_fwd * d * f + 4 * d * f + 2 * b * f + 10 * f * half, (n_fwd + 1) * b * f))(
-            h, w1f, *(w2f if mixing else (w2f,)), target, w1h, w2h)
+            h, w1f, *((*w2f, even) if mixing else (w2f,)), target, w1h, w2h)
 
 
 def tail_body(nt, mixing, loss_scale, *refs):
     refs = list(refs)
     a_ref, h_ref, hc_ref, t_ref, e0_ref, w1_ref, w20_ref = [refs.pop(0) for _ in range(7)]
-    w21_refs = [refs.pop(0) for _ in range(4 if mixing else 1)]
+    w21_refs = [refs.pop(0) for _ in range(5 if mixing else 1)]
     e1_ref, dz_ref, q_ref, wire_ref = [refs.pop(0) for _ in range(4)]
     if mixing:
         p_ref = refs.pop(0)
@@ -229,19 +232,20 @@
     i = pl.program_id(0)
     j = lax.rem(i, nt)
     blocks = row_blocks(h_ref.shape[0])
+    thin = row_blocks(h_ref.shape[0], THIN)
     half = e0_ref.shape[1]
 
     @pl.when(i == 0)
     def _():
         acc_scr[...] = jnp.zeros_like(acc_scr)
-        for r in blocks:
+        for r in thin:
             x = h_ref[r, :].astype(F32)
             n_scr[r, :] = (x * inv_rms_of(x)).astype(BF16)
 
     @pl.when(i < nt)
     def _():
         if mixing:
-            w2 = mix_vals(*[w[...] for w in w21_refs])
+            w2 = mix_refs(w21_refs)
             p_ref[...] = w2
         else:
             w2 = w21_refs[0][...]
@@ -252,7 +256,7 @@
 
     @pl.when(i == nt - 1)
     def _():
-        for r in blocks:
+        for r in thin:
             out = (hc_ref[r, :].astype(F32) + acc_scr[r, :]).astype(BF16)
             e = loss_scale * (out.astype(F32) - t_ref[r, :].astype(F32))
             e1_ref[r, :] = e
@@ -271,7 +275,7 @@
         wire_ref[...] = q.astype(BF16)
 
 
-def tail(act, h, hk, target, tk, e0, w1, k1, w20, k20, w21, k21, c21, half, loss_scale):
+def tail(act, h, hk, target, tk, e0, w1, k1, w20, k20, w21, k21, c21, half, loss_scale, even):
     b, d = h.shape[1:]
     f = w1.shape[2]
     nt = f // TILE
@@ -288,7 +292,7 @@
                 pl.BlockSpec((b, half), lambda i: (0, 0)), pl.BlockSpec((None, d, TILE), lambda i: (k1, 0, g_tile(i))),
                 pl.BlockSpec((None, TILE, half), lambda i: (k20, p_tile(i), 0))]
     if mixing:
-        in_specs += [pl.BlockSpec((TILE, half), lambda i: (p_tile(i), 0))] * 4
+        in_specs += [pl.BlockSpec((TILE, half), lambda i: (p_tile(i), 0))] * 4 + [pl.BlockSpec(memory_space=pltpu.SMEM)]
     else:
         in_specs.append(pl.BlockSpec((None, TILE, half), lambda i: (k21, p_tile(i), c21)))
     out_specs = [pl.BlockSpec((b, half), lambda i: (0, 0)), pl.BlockSpec((b, TILE), lambda i: (0, g_tile(i)))]
@@ -304,12 +308,12 @@
         scratch_shapes=[pltpu.VMEM((b, d), BF16), pltpu.VMEM((b, half), F32), pltpu.VMEM((nt, TILE, d), BF16), pltpu.VMEM((b, d), BF16)],
         compiler_params=params(),
         cost_estimate=cost(2 * b * f * (3 * d + half), 10 * d * f + 8 * f * half + 4 * b * f, b * f))(
-            act, h, h, target, e0, w1, w20, *(w21 if mixing else (w21,)))
+            act, h, h, target, e0, w1, w20, *((*w21, even) if mixing else (w21,)))
 
 
 def last_body(a_ref, dz_ref, h_ref, e0_ref, e1_ref, w1_ref, w2_ref, q_ref, wire_ref, en_ref, m_scr, elo_scr):
     j = pl.program_id(0)
-    blocks = row_blocks(h_ref.shape[0])
+    thin = row_blocks(h_ref.shape[0], THIN)
     half = e0_ref.shape[1]
 
     @pl.when(j == 0)
@@ -324,7 +328,7 @@
 
     @pl.when(j == pl.num_programs(0) - 1)
     def _():
-        for r in blocks:
+        for r in thin:
             step = norm_back(h_ref[r, :].astype(F32), m_scr[r, :])
             en_ref[r, :half] = e0_ref[r, :] + step[:, :half]
             en_ref[r, half:] = e1_ref[r, :] + step[:, half:]
@@ -351,10 +355,11 @@
         elo_scr, n_scr, a_scr, dz_scr = rest
     j = pl.program_id(0)
     blocks = row_blocks(h_ref.shape[0])
+    thin = row_blocks(h_ref.shape[0], THIN)
 
     @pl.when(j == 0)
     def _():
-        for r in blocks:
+        for r in thin:
             elo_scr[r, :] = e_ref[r, :].astype(BF16)
             x = h_ref[r, :].astype(F32)
             n_scr[r, :] = (x * inv_rms_of(x)).astype(BF16)
@@ -380,7 +385,7 @@
     if with_next:
         @pl.when(j == pl.num_programs(0) - 1)
         def _():
-            for r in blocks:
+            for r in thin:
                 en_ref[r, :] = e_ref[r, :] + norm_back(h_ref[r, :].astype(F32), m_scr[r, :])
 
 
@@ -404,29 +409,34 @@
         cost_estimate=cost(2 * n_mm * b * d * f, 20 * d * f, b * f))(e, h, w1, w2)
 
 
-def mix_vals(own, prev, nxt, row):
+def mix_vals(own, lead, trail, near, even, direct):
+    row, far = jnp.where(direct, lead, trail), jnp.where(direct, trail, lead)
+    first, second = jnp.where(even, far, near), jnp.where(even, near, far)
     row = row.astype(F32)
-    return (own + prev.astype(F32) + nxt.astype(F32) + row + row) / 5.0
-
-
-def place_body(n_alias, own_ref, prev_ref, nxt_ref, row_ref, *rest):
-    out_ref = rest[n_alias]
-    out_ref[...] = mix_vals(own_ref[...], prev_ref[...], nxt_ref[...], row_ref[...])
-
-
-def place(stack, shape, layer, col, own, recv):
+    return (own + first.astype(F32) + second.astype(F32) + row + row) / 5.0
+
+
+def mix_refs(refs):
+    return mix_vals(*[r[...] for r in refs[:4]], refs[4][0] == 1, refs[4][1] == 1)
+
+
+def place_body(own_ref, lead_ref, trail_ref, near_ref, sel_ref, *rest):
+    rest[-1][...] = mix_refs([own_ref, lead_ref, trail_ref, near_ref, sel_ref])
+
+
+def place(stack, shape, layer, col, own, recv, even):
     r, c = own.shape
     tr = r // 4
     spec = pl.BlockSpec((tr, c), lambda i: (i, 0))
-    args = [own, *recv]
-    in_specs = [spec] * 4
+    args = [own, *recv, even]
+    in_specs = [spec] * 4 + [pl.BlockSpec(memory_space=pltpu.SMEM)]
     aliases = {}
     if stack is not None:
         args.append(stack)
         in_specs.append(pl.BlockSpec(memory_space=pl.ANY))
-        aliases = {4: 0}
+        aliases = {5: 0}
     return pl.pallas_call(
-        functools.partial(place_body, len(aliases)), grid=(4,), in_specs=in_specs,
+        place_body, grid=(4,), in_specs=in_specs,
         out_specs=pl.BlockSpec((None, tr, c), lambda i: (layer, i, col)), out_shape=jax.ShapeDtypeStruct(shape, F32),
         input_output_aliases=aliases, compiler_params=params(), name='place',
         cost_estimate=cost(5 * r * c, 14 * r * c))(*args)
@@ -435,18 +445,26 @@
 def solution(mesh):
     n_rows = mesh.shape['row']
     n_cols = mesh.shape['col']
-    from_col_prev = [(i, (i + 1) % n_cols) for i in range(n_cols)]
-    from_col_next = [(i, (i - 1) % n_cols) for i in range(n_cols)]
-    from_row = [(i, (i + 1) % n_rows) for i in range(n_rows)]
+    near_pairs = [(i, i + 1 - 2 * (i % 2)) for i in range(n_cols)]
+    far_pairs = [(i, (i - 1 + 2 * (i % 2)) % n_cols) for i in range(n_cols)]
+    lead_pairs, trail_pairs = [], []
+    for r in range(n_rows):
+        for c, far in far_pairs:
+            here, across, other = r * n_cols + c, (r + 1) % n_rows * n_cols + c, r * n_cols + far
+            lead_pairs.append((here, across if c % 4 in (1, 2) else other))
+            trail_pairs.append((here, other if c % 4 in (1, 2) else across))
+
+    def lo_copy(weight):
+        return weight[0].astype(BF16)
 
     def after(value, *others):
         return lax.optimization_barrier((value,) + others)[0]
 
     def send(wire):
-        row = lax.ppermute(wire, 'row', from_row)
-        prev = lax.ppermute(wire, 'col', from_col_prev)
-        nxt = lax.ppermute(wire, 'col', from_col_next)
-        return prev, nxt, row
+        lead = lax.ppermute(wire, ('row', 'col'), lead_pairs)
+        trail = lax.ppermute(wire, ('row', 'col'), trail_pairs)
+        near = lax.ppermute(wire, 'col', near_pairs)
+        return lead, trail, near
 
     def device_fn(w_one, w_two, inputs, targets):
         n_layers, d, _ = w_one.shape[2:]
@@ -456,6 +474,8 @@
         loss_scale = 2.0 / (b * d)
         stack_one, stack_two = w_one[0, 0], w_two[0, 0]
         x_all, t_all = inputs[0, 0], targets[0, 0]
+        col = lax.axis_index('col')
+        even = jnp.stack([1 - col % 2, (col + 1) // 2 % 2]).astype(jnp.int32)
         one = [(stack_one, k) for k in range(n_layers)]
         two = [(stack_two, k) for k in range(last)]
         halves = [(stack_two, last), (stack_two, last, 1)]
@@ -466,10 +486,10 @@
             def settle(k):
                 name = names[k]
                 if name[0] == 'one':
-                    outs['one'] = place(outs.get('one'), stack_one.shape, name[1], 0, own[name], recvs[k])
+                    outs['one'] = place(outs.get('one'), stack_one.shape, name[1], 0, own[name], recvs[k], even)
                 else:
                     layer, col = (last, int(name[1])) if name[0] == 'h' else (name[1], 0)
-                    outs['two'] = place(outs.get('two'), stack_two.shape, layer, col, own[name], recvs[k])
+                    outs['two'] = place(outs.get('two'), stack_two.shape, layer, col, own[name], recvs[k], even)
 
             def push(name, q, wire, gate=None):
                 if gate is not None and final:
@@ -485,16 +505,16 @@
 
             hidden = [(x_all, step)]
             if step == 0:
-                hist, act, e0, q, wire = chain(last, *hidden[0], t_all, step, stack_one, 0, stack_two, 0, stack_one, last, stack_two, last, half, loss_scale)
+                hist, act, e0, q, wire = chain(last, *hidden[0], t_all, step, stack_one, 0, stack_two, 0, stack_one, last, stack_two, last, half, loss_scale, even, 2 * TILE)
                 hidden += [(hist, l) for l in range(last)]
             else:
                 for l in range(last - 1):
                     hidden.append((fwd_layer(*hidden[l], *one[l], *two[l])[None], 0))
-                hist, act, e0, q, wire, mixed_two = chain(1, *hidden[last - 1], t_all, step, *one[last - 1], two[last - 1], 0, *one[last], *halves[0], half, loss_scale)
+                hist, act, e0, q, wire, mixed_two = chain(1, *hidden[last - 1], t_all, step, lo_copy(one[last - 1]), 0, two[last - 1], 0, lo_copy(one[last]), 0, *halves[0], half, loss_scale, even, TILE)
                 two[last - 1] = (mixed_two[None], 0)
                 hidden.append((hist, 0))
             push('h0', q, wire)
-            res = tail(act, *hidden[last], t_all, step, e0, *one[last], *halves[0], *halves[1], half, loss_scale)
+            res = tail(act, *hidden[last], t_all, step, e0, *one[last], *halves[0], *halves[1], half, loss_scale, even)
             e1, dz = res[:2]
             push(('one', last), *res[2:4])
             if step > 0:
@@ -514,7 +534,7 @@
             if not final:
                 parts = {name: (own[name], *recv) for name, recv in zip(names, recvs)}
                 deferred = ('h1', ('two', last - 1))
-                mixed = {name: mix_vals(*vals)[None] for name, vals in parts.items() if name not in deferred}
+                mixed = {name: mix_vals(*vals, even[0] == 1, even[1] == 1)[None] for name, vals in parts.items() if name not in deferred}
                 one = [(mixed['one', l], 0) for l in range(n_layers)]
                 two = [(mixed['two', l], 0) for l in range(last - 1)] + [parts['two', last - 1]]
                 halves = [(mixed['h0'], 0), (parts['h1'], 0, 0)]

time: 1330 us -> 1220 us (0.917)
  waiting for transfers between devices: 712 us -> 612 us
  Pallas kernels: 411 us -> 439 us
  starting transfers between devices: 101 us -> 74.5 us
    ppermute x81, waiting for transfers between devices: 712 us -> 612 us  [the longest x27 375 us: send(): lead = lax.ppermute(wire, ('row', 'col'), lead_pairs)]
    ppermute x81, starting transfers between devices: 101 us -> 74.5 us  [the longest x27 29.6 us: send(): trail = lax.ppermute(wire, ('row', 'col'), trail_pairs)]
  transfers between devices with their start and end apart: 81 -> 81, of which waited for: 39 -> 31; matrix products, arithmetic and copies ran while one was open for 6% -> 7% of each run, Pallas kernels for 24% -> 32%
where the time goes in v1:
time: 1220 us; the launch traced here: 1210 us
  waiting for transfers between devices  612 us (50%)
  Pallas kernels  439 us (36%)
  other arithmetic  79.7 us (7%)
  starting transfers between devices  74.5 us (6%)
    ppermute x27, waiting for transfers between devices, send(): lead = lax.ppermute(wire, ('row', 'col'), lead_pairs)  375 us
    ppermute x27, waiting for transfers between devices, send(): trail = lax.ppermute(wire, ('row', 'col'), trail_pairs)  237 us
    pallas_call x9, Pallas kernels, bwd_layer(): pl.pallas_call(functools.partial(bwd_body, with_next), grid=(f // TILE,),...  173 us
    broadcast_in_dim x14, other arithmetic, device_fn(): mix_vals(*vals, even[0] == 1, even[1] == 1)[None]  79.1 us
    pallas_call x3, Pallas kernels, chain(): pl.pallas_call(functools.partial(chain_body, n_fwd, nt, mixing, loss_scal...  78.6 us
    pallas_call x3, Pallas kernels, tail(): pl.pallas_call(functools.partial(tail_body, nt, mixing, loss_scale), grid...  57.8 us
    pallas_call x9, Pallas kernels, place(): pl.pallas_call(place_body, grid=(4,), in_specs=in_specs, out_specs=pl.Blo...  55.9 us
    pallas_call x4, Pallas kernels, fwd_layer(): pl.pallas_call(fwd_body, grid=(f // TILE,), name='fwd', in_specs=[pl.Bloc...  38.3 us
  transfers between devices with their start and end apart: 81, of which 31 were waited for; matrix products, arithmetic and copies ran while one was open for 7% of the time, Pallas kernels for 32%

profile of v1, /device:TPU:0, one launch (start us, length us, event | category | flops | bytes accessed | tf_op | source)
XLA Modules:
  0.0 1213.1 jit_solution(11575253276613013505)
XLA Ops:
  0.6 32.3 %chain.3 = (bf16[3,1024,512]{2,1,0:T(8,128)(2,1)}, bf16[1024,2048]{1,0:T(8,128)(2,1)}, f32[1024,256]{1,0:T(8,128)}, f32[2048,256]{1,0:T(8,128)}, bf16[2048,256]{1,0:T(8,128)(2,1)}) custom-call(bf16[3,1024,512]{2,1,0:T(8,128)(2,1)} %bitcast.75, f32[4,512,2048]{2,1,0:T(8,128)} %bitcast.61, f32[4,2048,512]{2,1,0:T(8,128)} %bitcast.52, ...), custom_call_target="tpu_custom_call" | custom-call | flops 17179869184 | bytes 38797312 | tf_op jit(solution)/shard_map/chain/pallas_call | solution.py:214
  38.2 17.8 %tail.3 = (f32[1024,256]{1,0:T(8,128)}, bf16[1024,2048]{1,0:T(8,128)(2,1)}, f32[512,2048]{1,0:T(8,128)}, bf16[512,2048]{1,0:T(8,128)(2,1)}) custom-call(bf16[1024,2048]{1,0:T(8,128)(2,1)} %get-tuple-element.118.refs_0_.a_ref, bf16[3,1024,512]{2,1,0:T(8,128)(2,1)} %get-tuple-element.119.refs_1_.refs_2_.h_ref, ...), custom_call_target="tpu_custom_call" | custom-call | flops 7516192768 | bytes 23068672 | tf_op jit(solution)/shard_map/tail/pallas_call | solution.py:305
  69.2 21.0 %bwd_mid.6 = (f32[512,2048]{1,0:T(8,128)}, bf16[512,2048]{1,0:T(8,128)(2,1)}, f32[2048,512]{1,0:T(8,128)}, bf16[2048,512]{1,0:T(8,128)(2,1)}, f32[1024,512]{1,0:T(8,128)}) custom-call(f32[1024,512]{1,0:T(8,128)} %get-tuple-element.123.e_ref, bf16[3,1024,512]{2,1,0:T(8,128)(2,1)} %get-tuple-element.119.refs_1_.refs_2_.h_ref, f32[4,512,2048]{2,1,0:T(8,128)} %bitcast.65, ...), custom_call_target="tpu_custom_call" | custom-call | flops 10737418240 | bytes 20971520 | tf_op jit(solution)/shard_map/bwd_mid/pallas_call | solution.py:404
  91.8 20.4 %bwd_mid.7 = (f32[512,2048]{1,0:T(8,128)}, bf16[512,2048]{1,0:T(8,128)(2,1)}, f32[2048,512]{1,0:T(8,128)}, bf16[2048,512]{1,0:T(8,128)(2,1)}, f32[1024,512]{1,0:T(8,128)}) custom-call(f32[1024,512]{1,0:T(8,128)} %get-tuple-element.124.e_ref, bf16[3,1024,512]{2,1,0:T(8,128)(2,1)} %get-tuple-element.119.refs_1_.refs_2_.h_ref, f32[4,512,2048]{2,1,0:T(8,128)} %bitcast.66, ...), custom_call_target="tpu_custom_call" | custom-call | flops 10737418240 | bytes 20971520 | tf_op jit(solution)/shard_map/bwd_mid/pallas_call | solution.py:404
  113.5 16.6 %bwd_first.3 = (f32[512,2048]{1,0:T(8,128)}, bf16[512,2048]{1,0:T(8,128)(2,1)}, f32[2048,512]{1,0:T(8,128)}, bf16[2048,512]{1,0:T(8,128)(2,1)}) custom-call(f32[1024,512]{1,0:T(8,128)} %get-tuple-element.125.e_ref, bf16[3,1024,512]{2,1,0:T(8,128)(2,1)} %bitcast.76, f32[4,512,2048]{2,1,0:T(8,128)} %bitcast.67, f32[4,2048,512]{2,1,0:T(8,128)} %bitcast.59), custom_call_target="tpu_custom_call" | custom-call | flops 8589934592 | bytes 20971520 | tf_op jit(solution)/shard_map/bwd_first/pallas_call | solution.py:404
  141.7 19.8 %collective-permute-done.9 = bf16[512,2048]{1,0:T(8,128)(2,1)} collective-permute-done((bf16[512,2048]{1,0:T(8,128)(2,1)}, bf16[512,2048]{1,0:T(8,128)(2,1)}, u32[]{:S(2)}, u32[]{:S(2)}) %collective-permute-start.9) | collective-permute-done | bytes 2097184 | tf_op jit(solution)/shard_map/ppermute | solution.py:464
  164.4 19.0 %collective-permute-done.3 = bf16[512,2048]{1,0:T(8,128)(2,1)S(1)} collective-permute-done((bf16[512,2048]{1,0:T(8,128)(2,1)}, bf16[512,2048]{1,0:T(8,128)(2,1)S(1)}, u32[]{:S(2)}, u32[]{:S(2)}) %collective-permute-start.3) | collective-permute-done | bytes 2097184 | tf_op jit(solution)/shard_map/ppermute | solution.py:465
  191.0 15.4 %collective-permute-done.4 = bf16[512,2048]{1,0:T(8,128)(2,1)} collective-permute-done((bf16[512,2048]{1,0:T(8,128)(2,1)}, bf16[512,2048]{1,0:T(8,128)(2,1)}, u32[]{:S(2)}, u32[]{:S(2)}) %collective-permute-start.4) | collective-permute-done | bytes 2097184 | tf_op jit(solution)/shard_map/ppermute | solution.py:464
  281.7 14.5 %collective-permute-done.16 = bf16[512,2048]{1,0:T(8,128)(2,1)S(1)} collective-permute-done((bf16[512,2048]{1,0:T(8,128)(2,1)S(1)}, bf16[512,2048]{1,0:T(8,128)(2,1)S(1)}, u32[]{:S(2)}, u32[]{:S(2)}) %collective-permute-start.16) | collective-permute-done | bytes 2097184 | tf_op jit(solution)/shard_map/ppermute | solution.py:464
  350.4 35.8 %collective-permute-done.21.refs_3_ = bf16[2048,512]{1,0:T(8,128)(2,1)} collective-permute-done((bf16[2048,512]{1,0:T(8,128)(2,1)}, bf16[2048,512]{1,0:T(8,128)(2,1)}, u32[]{:S(2)}, u32[]{:S(2)}) %collective-permute-start.21) | collective-permute-done | bytes 2097184 | tf_op jit(solution)/shard_map/ppermute | solution.py:464
  395.8 23.0 %chain.4 = (bf16[1,1024,512]{2,1,0:T(8,128)(2,1)}, bf16[1024,2048]{1,0:T(8,128)(2,1)}, f32[1024,256]{1,0:T(8,128)}, f32[2048,256]{1,0:T(8,128)}, bf16[2048,256]{1,0:T(8,128)(2,1)}, /*index=5*/f32[2048,512]{1,0:T(8,128)}) custom-call(bf16[1,1024,512]{2,1,0:T(8,128)(2,1)} %bitcast.89, bf16[1,512,2048]{2,1,0:T(8,128)(2,1)} %get-tuple-element.239.refs_1_, ...), custom_call_target="tpu_custom_call" | custom-call | flops 8589934592 | bytes 22020096 | tf_op jit(solution)/shard_map/chain/pallas_call | solution.py:214
  421.4 20.1 %tail.4 = (f32[1024,256]{1,0:T(8,128)}, bf16[1024,2048]{1,0:T(8,128)(2,1)}, f32[512,2048]{1,0:T(8,128)}, bf16[512,2048]{1,0:T(8,128)(2,1)}, f32[2048,256]{1,0:T(8,128)}) custom-call(bf16[1024,2048]{1,0:T(8,128)(2,1)} %get-tuple-element.148.refs_0_.a_ref, bf16[1,1024,512]{2,1,0:T(8,128)(2,1)} %get-tuple-element.149.refs_1_.refs_2_.h_ref, ...), custom_call_target="tpu_custom_call" | custom-call | flops 7516192768 | bytes 23068672 | tf_op jit(solution)/shard_map/tail/pallas_call | solution.py:305
  455.2 20.5 %bwd_mid.8 = (f32[512,2048]{1,0:T(8,128)}, bf16[512,2048]{1,0:T(8,128)(2,1)}, f32[2048,512]{1,0:T(8,128)}, bf16[2048,512]{1,0:T(8,128)(2,1)}, f32[1024,512]{1,0:T(8,128)}) custom-call(f32[1024,512]{1,0:T(8,128)} %get-tuple-element.157.e_ref, bf16[1,1024,512]{2,1,0:T(8,128)(2,1)} %bitcast.90, f32[1,512,2048]{2,1,0:T(8,128)} %get-tuple-element.238.w1_ref, ...), custom_call_target="tpu_custom_call" | custom-call | flops 10737418240 | bytes 20971520 | tf_op jit(solution)/shard_map/bwd_mid/pallas_call | solution.py:404
  477.2 20.6 %bwd_mid.9 = (f32[512,2048]{1,0:T(8,128)}, bf16[512,2048]{1,0:T(8,128)(2,1)}, f32[2048,512]{1,0:T(8,128)}, bf16[2048,512]{1,0:T(8,128)(2,1)}, f32[1024,512]{1,0:T(8,128)}) custom-call(f32[1024,512]{1,0:T(8,128)} %get-tuple-element.159.e_ref, bf16[1,1024,512]{2,1,0:T(8,128)(2,1)} %bitcast.88, f32[1,512,2048]{2,1,0:T(8,128)} %fusion.5.w1_ref, ...), custom_call_target="tpu_custom_call" | custom-call | flops 10737418240 | bytes 20971520 | tf_op jit(solution)/shard_map/bwd_mid/pallas_call | solution.py:404
  499.0 16.5 %bwd_first.4 = (f32[512,2048]{1,0:T(8,128)}, bf16[512,2048]{1,0:T(8,128)(2,1)}, f32[2048,512]{1,0:T(8,128)}, bf16[2048,512]{1,0:T(8,128)(2,1)}) custom-call(f32[1024,512]{1,0:T(8,128)} %get-tuple-element.160.e_ref, bf16[3,1024,512]{2,1,0:T(8,128)(2,1)} %bitcast.78, f32[1,512,2048]{2,1,0:T(8,128)} %fusion.1.w1_ref, f32[1,2048,512]{2,1,0:T(8,128)} %fusion.3.w2_ref), custom_call_target="tpu_custom_call" | custom-call | flops 8589934592 | bytes 20971520 | tf_op jit(solution)/shard_map/bwd_first/pallas_call | solution.py:404
  524.2 22.4 %collective-permute-done.37 = bf16[512,2048]{1,0:T(8,128)(2,1)} collective-permute-done((bf16[512,2048]{1,0:T(8,128)(2,1)}, bf16[512,2048]{1,0:T(8,128)(2,1)}, u32[]{:S(2)}, u32[]{:S(2)}) %collective-permute-start.37) | collective-permute-done | bytes 2097184 | tf_op jit(solution)/shard_map/ppermute | solution.py:465
  548.1 43.3 %collective-permute-done.30 = bf16[512,2048]{1,0:T(8,128)(2,1)S(1)} collective-permute-done((bf16[512,2048]{1,0:T(8,128)(2,1)}, bf16[512,2048]{1,0:T(8,128)(2,1)S(1)}, u32[]{:S(2)}, u32[]{:S(2)}) %collective-permute-start.30) | collective-permute-done | bytes 2097184 | tf_op jit(solution)/shard_map/ppermute | solution.py:465
  603.1 33.3 %collective-permute-done.39 = bf16[2048,512]{1,0:T(8,128)(2,1)S(1)} collective-permute-done((bf16[2048,512]{1,0:T(8,128)(2,1)}, bf16[2048,512]{1,0:T(8,128)(2,1)S(1)}, u32[]{:S(2)}, u32[]{:S(2)}) %collective-permute-start.39) | collective-permute-done | bytes 2097184 | tf_op jit(solution)/shard_map/ppermute | solution.py:465
  647.7 33.6 %collective-permute-done.42 = bf16[512,2048]{1,0:T(8,128)(2,1)S(1)} collective-permute-done((bf16[512,2048]{1,0:T(8,128)(2,1)}, bf16[512,2048]{1,0:T(8,128)(2,1)S(1)}, u32[]{:S(2)}, u32[]{:S(2)}) %collective-permute-start.42) | collective-permute-done | bytes 2097184 | tf_op jit(solution)/shard_map/ppermute | solution.py:465
  699.2 27.2 %collective-permute-done.45 = bf16[2048,512]{1,0:T(8,128)(2,1)} collective-permute-done((bf16[2048,512]{1,0:T(8,128)(2,1)}, bf16[2048,512]{1,0:T(8,128)(2,1)}, u32[]{:S(2)}, u32[]{:S(2)}) %collective-permute-start.45) | collective-permute-done | bytes 2097184 | tf_op jit(solution)/shard_map/ppermute | solution.py:465
  770.8 23.3 %chain.5 = (bf16[1,1024,512]{2,1,0:T(8,128)(2,1)}, bf16[1024,2048]{1,0:T(8,128)(2,1)}, f32[1024,256]{1,0:T(8,128)}, f32[2048,256]{1,0:T(8,128)}, bf16[2048,256]{1,0:T(8,128)(2,1)}, /*index=5*/f32[2048,512]{1,0:T(8,128)}) custom-call(bf16[1,1024,512]{2,1,0:T(8,128)(2,1)} %bitcast.91, bf16[1,512,2048]{2,1,0:T(8,128)(2,1)} %get-tuple-element.235.refs_1_, ...), custom_call_target="tpu_custom_call" | custom-call | flops 8589934592 | bytes 22020096 | tf_op jit(solution)/shard_map/chain/pallas_call | solution.py:214
  794.1 19.9 %tail.5 = (f32[1024,256]{1,0:T(8,128)}, bf16[1024,2048]{1,0:T(8,128)(2,1)}, f32[512,2048]{1,0:T(8,128)}, bf16[512,2048]{1,0:T(8,128)(2,1)}, f32[2048,256]{1,0:T(8,128)}) custom-call(bf16[1024,2048]{1,0:T(8,128)(2,1)} %get-tuple-element.183.refs_0_.a_ref, bf16[1,1024,512]{2,1,0:T(8,128)(2,1)} %get-tuple-element.184.refs_1_.refs_2_.h_ref, ...), custom_call_target="tpu_custom_call" | custom-call | flops 7516192768 | bytes 23068672 | tf_op jit(solution)/shard_map/tail/pallas_call | solution.py:305
  830.5 53.4 %collective-permute-done.54.lead_ref = bf16[2048,256]{1,0:T(8,128)(2,1)S(1)} collective-permute-done((bf16[2048,256]{1,0:T(8,128)(2,1)}, bf16[2048,256]{1,0:T(8,128)(2,1)S(1)}, u32[]{:S(2)}, u32[]{:S(2)}) %collective-permute-start.54) | collective-permute-done | bytes 1048608 | tf_op jit(solution)/shard_map/ppermute | solution.py:464
  883.9 20.7 %bwd_mid.10 = (f32[512,2048]{1,0:T(8,128)}, bf16[512,2048]{1,0:T(8,128)(2,1)}, f32[2048,512]{1,0:T(8,128)}, bf16[2048,512]{1,0:T(8,128)(2,1)}, f32[1024,512]{1,0:T(8,128)}) custom-call(f32[1024,512]{1,0:T(8,128)} %get-tuple-element.193.e_ref, bf16[1,1024,512]{2,1,0:T(8,128)(2,1)} %bitcast.92, f32[1,512,2048]{2,1,0:T(8,128)} %get-tuple-element.234.w1_ref, ...), custom_call_target="tpu_custom_call" | custom-call | flops 10737418240 | bytes 20971520 | tf_op jit(solution)/shard_map/bwd_mid/pallas_call | solution.py:404
  912.5 20.4 %bwd_mid.11 = (f32[512,2048]{1,0:T(8,128)}, bf16[512,2048]{1,0:T(8,128)(2,1)}, f32[2048,512]{1,0:T(8,128)}, bf16[2048,512]{1,0:T(8,128)(2,1)}, f32[1024,512]{1,0:T(8,128)}) custom-call(f32[1024,512]{1,0:T(8,128)} %get-tuple-element.195.e_ref, bf16[1,1024,512]{2,1,0:T(8,128)(2,1)} %bitcast.86, f32[1,512,2048]{2,1,0:T(8,128)} %fusion.15.w1_ref, ...), custom_call_target="tpu_custom_call" | custom-call | flops 10737418240 | bytes 20971520 | tf_op jit(solution)/shard_map/bwd_mid/pallas_call | solution.py:404
  933.0 16.7 %bwd_first.5 = (f32[512,2048]{1,0:T(8,128)}, bf16[512,2048]{1,0:T(8,128)(2,1)}, f32[2048,512]{1,0:T(8,128)}, bf16[2048,512]{1,0:T(8,128)(2,1)}) custom-call(f32[1024,512]{1,0:T(8,128)} %get-tuple-element.197.e_ref, bf16[3,1024,512]{2,1,0:T(8,128)(2,1)} %bitcast.80, f32[1,512,2048]{2,1,0:T(8,128)} %fusion.11.w1_ref, f32[1,2048,512]{2,1,0:T(8,128)} %fusion.13.w2_ref), custom_call_target="tpu_custom_call" | custom-call | flops 8589934592 | bytes 20971520 | tf_op jit(solution)/shard_map/bwd_first/pallas_call | solution.py:404
  967.8 37.4 %collective-permute-done.66.lead_ref = bf16[512,2048]{1,0:T(8,128)(2,1)} collective-permute-done((bf16[512,2048]{1,0:T(8,128)(2,1)}, bf16[512,2048]{1,0:T(8,128)(2,1)}, u32[]{:S(2)}, u32[]{:S(2)}) %collective-permute-start.66) | collective-permute-done | bytes 2097184 | tf_op jit(solution)/shard_map/ppermute | solution.py:464
  1014.0 36.2 %collective-permute-done.63.lead_ref = bf16[2048,512]{1,0:T(8,128)(2,1)} collective-permute-done((bf16[2048,512]{1,0:T(8,128)(2,1)}, bf16[2048,512]{1,0:T(8,128)(2,1)}, u32[]{:S(2)}, u32[]{:S(2)}) %collective-permute-start.63) | collective-permute-done | bytes 2097184 | tf_op jit(solution)/shard_map/ppermute | solution.py:464
  1058.9 36.2 %collective-permute-done.72.lead_ref = bf16[512,2048]{1,0:T(8,128)(2,1)} collective-permute-done((bf16[512,2048]{1,0:T(8,128)(2,1)}, bf16[512,2048]{1,0:T(8,128)(2,1)}, u32[]{:S(2)}, u32[]{:S(2)}) %collective-permute-start.72) | collective-permute-done | bytes 2097184 | tf_op jit(solution)/shard_map/ppermute | solution.py:464
  1103.8 36.2 %collective-permute-done.69.lead_ref = bf16[2048,512]{1,0:T(8,128)(2,1)} collective-permute-done((bf16[2048,512]{1,0:T(8,128)(2,1)}, bf16[2048,512]{1,0:T(8,128)(2,1)}, u32[]{:S(2)}, u32[]{:S(2)}) %collective-permute-start.69) | collective-permute-done | bytes 2097184 | tf_op jit(solution)/shard_map/ppermute | solution.py:464
  1148.8 36.2 %collective-permute-done.78.lead_ref = bf16[2048,512]{1,0:T(8,128)(2,1)} collective-permute-done((bf16[2048,512]{1,0:T(8,128)(2,1)}, bf16[2048,512]{1,0:T(8,128)(2,1)}, u32[]{:S(2)}, u32[]{:S(2)}) %collective-permute-start.78) | collective-permute-done | bytes 2097184 | tf_op jit(solution)/shard_map/ppermute | solution.py:464
  1192.6 14.7 %collective-permute-done.75.lead_ref = bf16[2048,256]{1,0:T(8,128)(2,1)S(1)} collective-permute-done((bf16[2048,256]{1,0:T(8,128)(2,1)}, bf16[2048,256]{1,0:T(8,128)(2,1)S(1)}, u32[]{:S(2)}, u32[]{:S(2)}) %collective-permute-start.75) | collective-permute-done | bytes 1048608 | tf_op jit(solution)/shard_map/ppermute | solution.py:464
  (216 shorter events, 387.2 us)
Async XLA Ops:
  56.6 73.4 %collective-permute-start.1 = (bf16[512,2048]{1,0:T(8,128)(2,1)}, bf16[512,2048]{1,0:T(8,128)(2,1)}, u32[]{:S(2)}, u32[]{:S(2)}) collective-permute-start(bf16[512,2048]{1,0:T(8,128)(2,1)} %get-tuple-element.128), channel_id=1, source_target_pairs={{0,8},{1,2},{2,1},{3,11},{4,12},{5,6},{6,5},{7,15},{8,0},{9,10},{1... | collective-permute-start | bytes 6291464 | tf_op jit(solution)/shard_map/ppermute | solution.py:465
  131.6 74.9 %collective-permute-start.4 = (bf16[512,2048]{1,0:T(8,128)(2,1)}, bf16[512,2048]{1,0:T(8,128)(2,1)}, u32[]{:S(2)}, u32[]{:S(2)}) collective-permute-start(bf16[512,2048]{1,0:T(8,128)(2,1)} %get-tuple-element.129), channel_id=1, source_target_pairs={{0,7},{1,9},{2,10},{3,4},{4,3},{5,13},{6,14},{7,0},{8,15},{9,1},{1... | collective-permute-start | bytes 6291464 | tf_op jit(solution)/shard_map/ppermute | solution.py:464
  163.7 87.6 %collective-permute-start.13 = (bf16[2048,512]{1,0:T(8,128)(2,1)}, bf16[2048,512]{1,0:T(8,128)(2,1)S(1)}, u32[]{:S(2)}, u32[]{:S(2)}) collective-permute-start(bf16[2048,512]{1,0:T(8,128)(2,1)} %get-tuple-element.135), channel_id=1, source_target_pairs={{0,7},{1,9},{2,10},{3,4},{4,3},{5,13},{6,14},{7,0},{8,15},{9,1},{1... | collective-permute-start | bytes 6291464 | tf_op jit(solution)/shard_map/ppermute | solution.py:464
  213.5 82.7 %collective-permute-start.16 = (bf16[512,2048]{1,0:T(8,128)(2,1)S(1)}, bf16[512,2048]{1,0:T(8,128)(2,1)S(1)}, u32[]{:S(2)}, u32[]{:S(2)}) collective-permute-start(bf16[512,2048]{1,0:T(8,128)(2,1)S(1)} %copy-done.18), channel_id=1, source_target_pairs={{0,7},{1,9},{2,10},{3,4},{4,3},{5,13},{6,14},{7,0},{8,15},{9,1},{1... | collective-permute-start | bytes 6291464 | tf_op jit(solution)/shard_map/ppermute | solution.py:464
  258.9 82.3 %collective-permute-start.19 = (bf16[2048,512]{1,0:T(8,128)(2,1)}, bf16[2048,512]{1,0:T(8,128)(2,1)}, u32[]{:S(2)}, u32[]{:S(2)}) collective-permute-start(bf16[2048,512]{1,0:T(8,128)(2,1)} %get-tuple-element.141), channel_id=1, source_target_pairs={{0,7},{1,9},{2,10},{3,4},{4,3},{5,13},{6,14},{7,0},{8,15},{9,1},{1... | collective-permute-start | bytes 6291464 | tf_op jit(solution)/shard_map/ppermute | solution.py:464
  298.8 87.4 %collective-permute-start.21 = (bf16[2048,512]{1,0:T(8,128)(2,1)}, bf16[2048,512]{1,0:T(8,128)(2,1)}, u32[]{:S(2)}, u32[]{:S(2)}) collective-permute-start(bf16[2048,512]{1,0:T(8,128)(2,1)} %get-tuple-element.145), channel_id=1, source_target_pairs={{0,7},{1,9},{2,10},{3,4},{4,3},{5,13},{6,14},{7,0},{8,15},{9,1},{1... | collective-permute-start | bytes 6291464 | tf_op jit(solution)/shard_map/ppermute | solution.py:464
  309.7 86.1 %collective-permute-start.22 = (bf16[2048,512]{1,0:T(8,128)(2,1)}, bf16[2048,512]{1,0:T(8,128)(2,1)}, u32[]{:S(2)}, u32[]{:S(2)}) collective-permute-start(bf16[2048,512]{1,0:T(8,128)(2,1)} %get-tuple-element.145), channel_id=1, source_target_pairs={{0,8},{1,2},{2,1},{3,11},{4,12},{5,6},{6,5},{7,15},{8,0},{9,10},{1... | collective-permute-start | bytes 6291464 | tf_op jit(solution)/shard_map/ppermute | solution.py:465
  318.4 77.4 %collective-permute-start.23 = (bf16[2048,512]{1,0:T(8,128)(2,1)}, bf16[2048,512]{1,0:T(8,128)(2,1)}, u32[]{:S(2)}, u32[]{:S(2)}) collective-permute-start(bf16[2048,512]{1,0:T(8,128)(2,1)} %get-tuple-element.145), channel_id=1, source_target_pairs={{0,1},{1,0},{2,3},{3,2},{4,5},{5,4},{6,7},{7,6},{8,9},{9,8},{10,11... | collective-permute-start | bytes 6291464 | tf_op jit(solution)/shard_map/ppermute | solution.py:466
  341.3 80.1 %collective-permute-start.24 = (bf16[2048,256]{1,0:T(8,128)(2,1)}, bf16[2048,256]{1,0:T(8,128)(2,1)}, u32[]{:S(2)}, u32[]{:S(2)}) collective-permute-start(bf16[2048,256]{1,0:T(8,128)(2,1)} %get-tuple-element.153), channel_id=1, source_target_pairs={{0,7},{1,9},{2,10},{3,4},{4,3},{5,13},{6,14},{7,0},{8,15},{9,1},{1... | collective-permute-start | bytes 3145736 | tf_op jit(solution)/shard_map/ppermute | solution.py:464
  342.4 79.0 %collective-permute-start.25 = (bf16[2048,256]{1,0:T(8,128)(2,1)}, bf16[2048,256]{1,0:T(8,128)(2,1)}, u32[]{:S(2)}, u32[]{:S(2)}) collective-permute-start(bf16[2048,256]{1,0:T(8,128)(2,1)} %get-tuple-element.153), channel_id=1, source_target_pairs={{0,8},{1,2},{2,1},{3,11},{4,12},{5,6},{6,5},{7,15},{8,0},{9,10},{1... | collective-permute-start | bytes 3145736 | tf_op jit(solution)/shard_map/ppermute | solution.py:465
  442.9 72.6 %collective-permute-start.28 = (bf16[512,2048]{1,0:T(8,128)(2,1)}, bf16[512,2048]{1,0:T(8,128)(2,1)}, u32[]{:S(2)}, u32[]{:S(2)}) collective-permute-start(bf16[512,2048]{1,0:T(8,128)(2,1)} %get-tuple-element.163), channel_id=1, source_target_pairs={{0,8},{1,2},{2,1},{3,11},{4,12},{5,6},{6,5},{7,15},{8,0},{9,10},{1... | collective-permute-start | bytes 6291464 | tf_op jit(solution)/shard_map/ppermute | solution.py:465
  515.5 76.0 %collective-permute-start.30 = (bf16[512,2048]{1,0:T(8,128)(2,1)}, bf16[512,2048]{1,0:T(8,128)(2,1)S(1)}, u32[]{:S(2)}, u32[]{:S(2)}) collective-permute-start(bf16[512,2048]{1,0:T(8,128)(2,1)} %get-tuple-element.164), channel_id=1, source_target_pairs={{0,8},{1,2},{2,1},{3,11},{4,12},{5,6},{6,5},{7,15},{8,0},{9,10},{1... | collective-permute-start | bytes 6291464 | tf_op jit(solution)/shard_map/ppermute | solution.py:465
  516.4 79.6 %collective-permute-start.31 = (bf16[512,2048]{1,0:T(8,128)(2,1)}, bf16[512,2048]{1,0:T(8,128)(2,1)S(1)}, u32[]{:S(2)}, u32[]{:S(2)}) collective-permute-start(bf16[512,2048]{1,0:T(8,128)(2,1)} %get-tuple-element.164), channel_id=1, source_target_pairs={{0,7},{1,9},{2,10},{3,4},{4,3},{5,13},{6,14},{7,0},{8,15},{9,1},{1... | collective-permute-start | bytes 6291464 | tf_op jit(solution)/shard_map/ppermute | solution.py:464
  546.6 89.8 %collective-permute-start.39 = (bf16[2048,512]{1,0:T(8,128)(2,1)}, bf16[2048,512]{1,0:T(8,128)(2,1)S(1)}, u32[]{:S(2)}, u32[]{:S(2)}) collective-permute-start(bf16[2048,512]{1,0:T(8,128)(2,1)} %get-tuple-element.170), channel_id=1, source_target_pairs={{0,8},{1,2},{2,1},{3,11},{4,12},{5,6},{6,5},{7,15},{8,0},{9,10},{1... | collective-permute-start | bytes 6291464 | tf_op jit(solution)/shard_map/ppermute | solution.py:465
  547.8 94.5 %collective-permute-start.40 = (bf16[2048,512]{1,0:T(8,128)(2,1)}, bf16[2048,512]{1,0:T(8,128)(2,1)S(1)}, u32[]{:S(2)}, u32[]{:S(2)}) collective-permute-start(bf16[2048,512]{1,0:T(8,128)(2,1)} %get-tuple-element.170), channel_id=1, source_target_pairs={{0,7},{1,9},{2,10},{3,4},{4,3},{5,13},{6,14},{7,0},{8,15},{9,1},{1... | collective-permute-start | bytes 6291464 | tf_op jit(solution)/shard_map/ppermute | solution.py:464
  596.0 85.4 %collective-permute-start.42 = (bf16[512,2048]{1,0:T(8,128)(2,1)}, bf16[512,2048]{1,0:T(8,128)(2,1)S(1)}, u32[]{:S(2)}, u32[]{:S(2)}) collective-permute-start(bf16[512,2048]{1,0:T(8,128)(2,1)} %get-tuple-element.173), channel_id=1, source_target_pairs={{0,8},{1,2},{2,1},{3,11},{4,12},{5,6},{6,5},{7,15},{8,0},{9,10},{1... | collective-permute-start | bytes 6291464 | tf_op jit(solution)/shard_map/ppermute | solution.py:465
  602.7 82.5 %collective-permute-start.43 = (bf16[512,2048]{1,0:T(8,128)(2,1)}, bf16[512,2048]{1,0:T(8,128)(2,1)S(1)}, u32[]{:S(2)}, u32[]{:S(2)}) collective-permute-start(bf16[512,2048]{1,0:T(8,128)(2,1)} %get-tuple-element.173), channel_id=1, source_target_pairs={{0,7},{1,9},{2,10},{3,4},{4,3},{5,13},{6,14},{7,0},{8,15},{9,1},{1... | collective-permute-start | bytes 6291464 | tf_op jit(solution)/shard_map/ppermute | solution.py:464
  642.3 84.1 %collective-permute-start.45 = (bf16[2048,512]{1,0:T(8,128)(2,1)}, bf16[2048,512]{1,0:T(8,128)(2,1)}, u32[]{:S(2)}, u32[]{:S(2)}) collective-permute-start(bf16[2048,512]{1,0:T(8,128)(2,1)} %get-tuple-element.176), channel_id=1, source_target_pairs={{0,8},{1,2},{2,1},{3,11},{4,12},{5,6},{6,5},{7,15},{8,0},{9,10},{1... | collective-permute-start | bytes 6291464 | tf_op jit(solution)/shard_map/ppermute | solution.py:465
  647.3 87.2 %collective-permute-start.46 = (bf16[2048,512]{1,0:T(8,128)(2,1)}, bf16[2048,512]{1,0:T(8,128)(2,1)}, u32[]{:S(2)}, u32[]{:S(2)}) collective-permute-start(bf16[2048,512]{1,0:T(8,128)(2,1)} %get-tuple-element.176), channel_id=1, source_target_pairs={{0,7},{1,9},{2,10},{3,4},{4,3},{5,13},{6,14},{7,0},{8,15},{9,1},{1... | collective-permute-start | bytes 6291464 | tf_op jit(solution)/shard_map/ppermute | solution.py:464
  698.2 72.6 %collective-permute-start.49 = (bf16[2048,512]{1,0:T(8,128)(2,1)}, bf16[2048,512]{1,0:T(8,128)(2,1)}, u32[]{:S(2)}, u32[]{:S(2)}) collective-permute-start(bf16[2048,512]{1,0:T(8,128)(2,1)} %get-tuple-element.180), channel_id=1, source_target_pairs={{0,8},{1,2},{2,1},{3,11},{4,12},{5,6},{6,5},{7,15},{8,0},{9,10},{1... | collective-permute-start | bytes 6291464 | tf_op jit(solution)/shard_map/ppermute | solution.py:465
  814.0 98.5 %collective-permute-start.60 = (bf16[512,2048]{1,0:T(8,128)(2,1)}, bf16[512,2048]{1,0:T(8,128)(2,1)}, u32[]{:S(2)}, u32[]{:S(2)}) collective-permute-start(bf16[512,2048]{1,0:T(8,128)(2,1)} %get-tuple-element.205), channel_id=1, source_target_pairs={{0,7},{1,9},{2,10},{3,4},{4,3},{5,13},{6,14},{7,0},{8,15},{9,1},{1... | collective-permute-start | bytes 6291464 | tf_op jit(solution)/shard_map/ppermute | solution.py:464
  816.7 132.9 %collective-permute-start.61 = (bf16[512,2048]{1,0:T(8,128)(2,1)}, bf16[512,2048]{1,0:T(8,128)(2,1)}, u32[]{:S(2)}, u32[]{:S(2)}) collective-permute-start(bf16[512,2048]{1,0:T(8,128)(2,1)} %get-tuple-element.205), channel_id=1, source_target_pairs={{0,8},{1,2},{2,1},{3,11},{4,12},{5,6},{6,5},{7,15},{8,0},{9,10},{1... | collective-permute-start | bytes 6291464 | tf_op jit(solution)/shard_map/ppermute | solution.py:465
  818.0 86.7 %collective-permute-start.55 = (bf16[2048,256]{1,0:T(8,128)(2,1)}, bf16[2048,256]{1,0:T(8,128)(2,1)}, u32[]{:S(2)}, u32[]{:S(2)}) collective-permute-start(bf16[2048,256]{1,0:T(8,128)(2,1)} %get-tuple-element.200), channel_id=1, source_target_pairs={{0,8},{1,2},{2,1},{3,11},{4,12},{5,6},{6,5},{7,15},{8,0},{9,10},{1... | collective-permute-start | bytes 3145736 | tf_op jit(solution)/shard_map/ppermute | solution.py:465
  818.8 85.9 %collective-permute-start.56 = (bf16[2048,256]{1,0:T(8,128)(2,1)}, bf16[2048,256]{1,0:T(8,128)(2,1)}, u32[]{:S(2)}, u32[]{:S(2)}) collective-permute-start(bf16[2048,256]{1,0:T(8,128)(2,1)} %get-tuple-element.200), channel_id=1, source_target_pairs={{0,1},{1,0},{2,3},{3,2},{4,5},{5,4},{6,7},{7,6},{8,9},{9,8},{10,11... | collective-permute-start | bytes 3145736 | tf_op jit(solution)/shard_map/ppermute | solution.py:466
  964.3 85.9 %collective-permute-start.63 = (bf16[2048,512]{1,0:T(8,128)(2,1)}, bf16[2048,512]{1,0:T(8,128)(2,1)}, u32[]{:S(2)}, u32[]{:S(2)}) collective-permute-start(bf16[2048,512]{1,0:T(8,128)(2,1)} %get-tuple-element.210), channel_id=1, source_target_pairs={{0,7},{1,9},{2,10},{3,4},{4,3},{5,13},{6,14},{7,0},{8,15},{9,1},{1... | collective-permute-start | bytes 6291464 | tf_op jit(solution)/shard_map/ppermute | solution.py:464
  965.9 85.2 %collective-permute-start.64 = (bf16[2048,512]{1,0:T(8,128)(2,1)}, bf16[2048,512]{1,0:T(8,128)(2,1)}, u32[]{:S(2)}, u32[]{:S(2)}) collective-permute-start(bf16[2048,512]{1,0:T(8,128)(2,1)} %get-tuple-element.210), channel_id=1, source_target_pairs={{0,8},{1,2},{2,1},{3,11},{4,12},{5,6},{6,5},{7,15},{8,0},{9,10},{1... | collective-permute-start | bytes 6291464 | tf_op jit(solution)/shard_map/ppermute | solution.py:465
  1012.8 82.3 %collective-permute-start.72 = (bf16[512,2048]{1,0:T(8,128)(2,1)}, bf16[512,2048]{1,0:T(8,128)(2,1)}, u32[]{:S(2)}, u32[]{:S(2)}) collective-permute-start(bf16[512,2048]{1,0:T(8,128)(2,1)} %get-tuple-element.221), channel_id=1, source_target_pairs={{0,7},{1,9},{2,10},{3,4},{4,3},{5,13},{6,14},{7,0},{8,15},{9,1},{1... | collective-permute-start | bytes 6291464 | tf_op jit(solution)/shard_map/ppermute | solution.py:464
  1013.6 82.4 %collective-permute-start.73 = (bf16[512,2048]{1,0:T(8,128)(2,1)}, bf16[512,2048]{1,0:T(8,128)(2,1)}, u32[]{:S(2)}, u32[]{:S(2)}) collective-permute-start(bf16[512,2048]{1,0:T(8,128)(2,1)} %get-tuple-element.221), channel_id=1, source_target_pairs={{0,8},{1,2},{2,1},{3,11},{4,12},{5,6},{6,5},{7,15},{8,0},{9,10},{1... | collective-permute-start | bytes 6291464 | tf_op jit(solution)/shard_map/ppermute | solution.py:465
  1057.8 82.3 %collective-permute-start.69 = (bf16[2048,512]{1,0:T(8,128)(2,1)}, bf16[2048,512]{1,0:T(8,128)(2,1)}, u32[]{:S(2)}, u32[]{:S(2)}) collective-permute-start(bf16[2048,512]{1,0:T(8,128)(2,1)} %get-tuple-element.219), channel_id=1, source_target_pairs={{0,7},{1,9},{2,10},{3,4},{4,3},{5,13},{6,14},{7,0},{8,15},{9,1},{1... | collective-permute-start | bytes 6291464 | tf_op jit(solution)/shard_map/ppermute | solution.py:464
  1058.6 82.4 %collective-permute-start.70 = (bf16[2048,512]{1,0:T(8,128)(2,1)}, bf16[2048,512]{1,0:T(8,128)(2,1)}, u32[]{:S(2)}, u32[]{:S(2)}) collective-permute-start(bf16[2048,512]{1,0:T(8,128)(2,1)} %get-tuple-element.219), channel_id=1, source_target_pairs={{0,8},{1,2},{2,1},{3,11},{4,12},{5,6},{6,5},{7,15},{8,0},{9,10},{1... | collective-permute-start | bytes 6291464 | tf_op jit(solution)/shard_map/ppermute | solution.py:465
  1102.7 82.3 %collective-permute-start.78 = (bf16[2048,512]{1,0:T(8,128)(2,1)}, bf16[2048,512]{1,0:T(8,128)(2,1)}, u32[]{:S(2)}, u32[]{:S(2)}) collective-permute-start(bf16[2048,512]{1,0:T(8,128)(2,1)} %get-tuple-element.232), channel_id=1, source_target_pairs={{0,7},{1,9},{2,10},{3,4},{4,3},{5,13},{6,14},{7,0},{8,15},{9,1},{1... | collective-permute-start | bytes 6291464 | tf_op jit(solution)/shard_map/ppermute | solution.py:464
  1103.5 82.4 %collective-permute-start.79 = (bf16[2048,512]{1,0:T(8,128)(2,1)}, bf16[2048,512]{1,0:T(8,128)(2,1)}, u32[]{:S(2)}, u32[]{:S(2)}) collective-permute-start(bf16[2048,512]{1,0:T(8,128)(2,1)} %get-tuple-element.232), channel_id=1, source_target_pairs={{0,8},{1,2},{2,1},{3,11},{4,12},{5,6},{6,5},{7,15},{8,0},{9,10},{1... | collective-permute-start | bytes 6291464 | tf_op jit(solution)/shard_map/ppermute | solution.py:465
  (69 other events, 2877.5 us)
